TPU v7x, 32 devices: a whole 2x2x4 slice. The times are simulated.
32 devices in a mesh: gx: 4 (over z), gy: 8 (over y, x, core).
Axes of the slice: x: 2, y: 2, z: 4, core: 2. Of those that a mesh axis runs over, the one named last changes fastest.
Arguments:
- prolong: bfloat16 [2048, 24, 128], P(('gx', 'gy')), may hold values from -0.5 to 0.5
- stiffness: bfloat16 [4096, 4, 128, 128], P(('gx', 'gy')), may hold values from -6 to 6
- request: int32 [4096], P(('gx', 'gy')), may hold values from 0 to 63, as said below
- col_slot: int32 [4096, 4], P(('gx', 'gy')), may hold values from 0 to 127
- col_pos: int32 [4096, 4], P(('gx', 'gy')), may hold values from 0 to 15, as said below
- coarse_owner: int32 [2048, 1], P(('gx', 'gy')), may hold values from 0 to 31; in each aligned block of 64 rows (0 to 63, 64 to 127, ...) at most 4 rows name the same one
Outputs:
- coarse: float32 [4096, 24, 384], P(('gx', 'gy'))
Inputs may be any that keep to these rules, and one draw needn't show every extreme that they name: `request`: on each device, entries k * 4 to (k + 1) * 4 - 1 name distinct aggregates of device k, as local indices there. `col_pos`: the 4 entries of one block row are distinct. `coarse_owner`: among one device's 64 aggregates at most 4 share a coarse owner, and on some devices 4 do.
All inputs are finite; a program needn't handle non-finite values.
Results may differ from a plain program's by a relative error of at most 0.0003.
Values may be sent and summed in bfloat16 or wider, within the bound.
A program may use at most 128 MiB of HBM per device.

v0:
```python
import functools

import jax
import jax.numpy as jnp
from jax import lax
from jax.experimental import pallas as pl
from jax.experimental.pallas import tpu as pltpu
from jax.sharding import PartitionSpec as P

MAXNB = 16
AXES = ("gx", "gy")
LANES = 128
TOP = 32767.0
MESH = pl.DeviceIdType.MESH
HBM = pl.BlockSpec(memory_space=pl.ANY)
VMEM = pl.BlockSpec(memory_space=pltpu.VMEM)
SMEM = pl.BlockSpec(memory_space=pltpu.SMEM)
NT = (((1,), (1,)), ((), ()))


def peer_at(k, gx, gy, mixed):
    n = gx * gy
    x, y = lax.axis_index("gx"), lax.axis_index("gy")
    if gx % 2:
        return lax.rem(x * gy + y + 1 + k, n)
    half = gx // 2
    count = half * gy
    if mixed:
        near, i = lax.rem(k, 2), k // 2
    else:
        near, i = k // count, lax.rem(k, count)
    i = lax.rem(i + near, count)
    side = lax.rem(x // half + 1 + near, 2)
    row = side * half + lax.rem(x + i // gy, half)
    return row * gy + lax.rem(y + i, gy)


def deliver_kernel(dims, code_ref, scale_ref, out_ref, land_ref, land_scale, wide_ref, *sems):
    gx, gy, cv = dims
    code_send, code_recv, scale_send, scale_recv, out_sem = sems
    n, rows, width = code_ref.shape
    take = rows // cv
    me = lax.axis_index("gx") * gy + lax.axis_index("gy")
    barrier = pltpu.get_barrier_semaphore()

    def where(peer):
        return (peer // gy, lax.rem(peer, gy))

    def greet(k, c):
        peer = peer_at(k, gx, gy, True)
        pl.semaphore_signal(barrier, inc=1, device_id=where(peer), device_id_type=MESH)
        return c

    lax.fori_loop(0, n - 1, greet, 0)

    def copies(peer, source):
        return [
            pltpu.make_async_remote_copy(
                src_ref=src.at[peer], dst_ref=dst.at[source],
                send_sem=send.at[peer], recv_sem=recv.at[source],
                device_id=where(peer), device_id_type=MESH,
            )
            for src, dst, send, recv in (
                (scale_ref, land_scale, scale_send, scale_recv),
                (code_ref, land_ref, code_send, code_recv),
            )
        ]

    def out_copy(p):
        at = pl.ds(p * take, take)
        return pltpu.make_async_copy(wide_ref.at[at], out_ref.at[at], out_sem.at[p])

    pl.semaphore_wait(barrier, n - 1)

    def send(k, c):
        for copy in copies(peer_at(k, gx, gy, True), me):
            copy.start()
        return c

    lax.fori_loop(0, n - 1, send, 0)

    def decode(code, scale, p):
        values = code.astype(jnp.int32).astype(jnp.float32) * as_column(scale, rows)
        wide_ref[pl.ds(p * take, take)] = values.reshape(take, cv, width)
        out_copy(p).start()

    decode(code_ref[me], scale_ref[me], me)

    def drain(k, c):
        source = peer_at(k, gx, gy, True)
        for copy in copies(source, source):
            copy.wait()
        decode(land_ref[source], land_scale[source], source)
        return c

    lax.fori_loop(0, n - 1, drain, 0)

    def finish(p, c):
        out_copy(p).wait()
        return c

    lax.fori_loop(0, n, finish, 0)


def delivered(code, scale, cv, gx, gy):
    n, rows, width = code.shape
    sem = pltpu.SemaphoreType.DMA
    out = (n * rows // cv, cv, width)
    return pl.pallas_call(
        functools.partial(deliver_kernel, (gx, gy, cv)),
        out_shape=jax.ShapeDtypeStruct(out, jnp.float32),
        in_specs=[VMEM, VMEM],
        out_specs=HBM,
        scratch_shapes=[
            pltpu.VMEM(code.shape, jnp.int16),
            pltpu.VMEM(scale.shape, jnp.float32),
            pltpu.VMEM(out, jnp.float32),
        ]
        + [sem((n,))] * 5,
        compiler_params=pltpu.CompilerParams(
            collective_id=4, has_side_effects=True, vmem_limit_bytes=40 << 20
        ),
        name="delivered",
    )(code, scale)


def exchange_kernel(gx, gy, count, *refs):
    ins, outs = refs[:count], refs[count : 2 * count]
    send_sem, recv_sem, local_sem = refs[2 * count :]
    n = gx * gy
    me = lax.axis_index("gx") * gy + lax.axis_index("gy")
    barrier = pltpu.get_barrier_semaphore()

    def greet(k, c):
        peer = lax.rem(me + k, n)
        pl.semaphore_signal(barrier, inc=1, device_id=(peer // gy, lax.rem(peer, gy)), device_id_type=MESH)
        return c

    lax.fori_loop(1, n, greet, 0)
    own = [pltpu.make_async_copy(ins[i].at[me], outs[i].at[me], local_sem.at[i]) for i in range(count)]
    for copy in own:
        copy.start()
    pl.semaphore_wait(barrier, n - 1)

    def copies(k, source):
        peer = lax.rem(me + k, n)
        return [
            pltpu.make_async_remote_copy(
                src_ref=ins[i].at[peer],
                dst_ref=outs[i].at[source],
                send_sem=send_sem.at[i, k],
                recv_sem=recv_sem.at[i, k],
                device_id=(peer // gy, lax.rem(peer, gy)),
                device_id_type=MESH,
            )
            for i in range(count)
        ]

    def send(k, c):
        for copy in copies(k, me):
            copy.start()
        return c

    lax.fori_loop(1, n, send, 0)

    def drain(k, c):
        for copy in copies(k, lax.rem(me + n - k, n)):
            copy.wait()
        return c

    lax.fori_loop(1, n, drain, 0)
    for copy in own:
        copy.wait()


def exchange(arrays, gx, gy, number):
    count = len(arrays)
    n = gx * gy
    return pl.pallas_call(
        functools.partial(exchange_kernel, gx, gy, count),
        out_shape=[jax.ShapeDtypeStruct(a.shape, a.dtype) for a in arrays],
        in_specs=[HBM] * count,
        out_specs=[HBM] * count,
        scratch_shapes=[
            pltpu.SemaphoreType.DMA((count, n)),
            pltpu.SemaphoreType.DMA((count, n)),
            pltpu.SemaphoreType.DMA((count,)),
        ],
        compiler_params=pltpu.CompilerParams(collective_id=number, has_side_effects=True),
        name=f"exchange{number}",
    )(*arrays)


def as_row(column):
    rows = column.shape[0]
    shape = (rows, LANES)
    eye = lax.broadcasted_iota(jnp.int32, shape, 0) == lax.broadcasted_iota(jnp.int32, shape, 1)
    return jnp.sum(jnp.where(eye, column, 0.0), axis=0, keepdims=True)


def as_column(row, rows):
    shape = (rows, LANES)
    eye = lax.broadcasted_iota(jnp.int32, shape, 0) == lax.broadcasted_iota(jnp.int32, shape, 1)
    return jnp.sum(jnp.where(eye, row, 0.0), axis=1, keepdims=True)


def coded(values):
    top = jnp.maximum(jnp.max(jnp.abs(values), axis=1, keepdims=True), 1e-30)
    code = jnp.round(values * (TOP / top)).astype(jnp.int32).astype(jnp.int16)
    return code, as_row(top * (1.0 / TOP))


def group_product(dims, grp, slot_ref, wide_ref, cols_ref, mats_of):
    cv, bps, group = dims
    dof = wide_ref.shape[-1]
    span = bps * cv
    lane = lax.broadcasted_iota(jnp.int32, (dof, LANES), 1)
    applied = []
    for tl in range(group):
        for q in range(bps):
            block = wide_ref[slot_ref[grp * group + tl, q]]
            at = (span * tl + cv * q) % LANES
            first = min(cv, LANES - at)
            cols_ref[tl, at : at + first, :] = block[:first]
            if first < cv:
                cols_ref[tl, 0 : cv - first, :] = block[first:]
    for tl in range(group):
        cols = cols_ref[tl].astype(jnp.bfloat16)
        mats = mats_of(tl).reshape(bps * dof, dof)
        prod = lax.dot_general(mats, cols, NT, preferred_element_type=jnp.float32)
        rel = (lane + (LANES * tl - span * tl) % LANES) % LANES
        one = prod[(bps - 1) * dof :]
        for q in range(bps - 2, -1, -1):
            one = jnp.where(rel < cv * (q + 1), prod[q * dof : (q + 1) * dof], one)
        applied.append(one)
    tiles = []
    for j in range(span * group // LANES):
        low, high = LANES * j // span, (LANES * (j + 1) - 1) // span
        tile = applied[high]
        for tl in range(high - 1, low - 1, -1):
            tile = jnp.where(lane < span * (tl + 1) - LANES * j, applied[tl], tile)
        tiles.append(tile)
    whole = jnp.concatenate(tiles, axis=1)
    hi = whole.astype(jnp.bfloat16)
    lo = (whole - hi.astype(jnp.float32)).astype(jnp.bfloat16)
    rows = wide_ref[pl.ds(grp * group, group)].reshape(group * cv, dof).astype(jnp.bfloat16)
    both = jnp.dot(rows, hi, preferred_element_type=jnp.float32) + jnp.dot(
        rows, lo, preferred_element_type=jnp.float32
    )
    wide_lane = lax.broadcasted_iota(jnp.int32, (cv, span * group), 1)
    out = both[(group - 1) * cv :]
    for tl in range(group - 2, -1, -1):
        out = jnp.where(wide_lane < span * (tl + 1), both[tl * cv : (tl + 1) * cv], out)
    return out


def product_kernel(dims, slot_ref, fetched_ref, stiff_ref, out_ref, wide_ref, cols_ref):
    cv, bps, group, per_step = dims
    step = pl.program_id(0)

    @pl.when(step == 0)
    def _():
        wide_ref[...] = fetched_ref[...].astype(jnp.float32)

    def body(k, c):
        out_ref[k] = group_product(
            (cv, bps, group), step * per_step + k, slot_ref, wide_ref, cols_ref,
            lambda tl: stiff_ref[k * group + tl],
        )
        return c

    lax.fori_loop(0, per_step, body, 0)


def products(fetched, stiffness, col_slot, group):
    slots, cv, dof = fetched.shape
    bps = stiffness.shape[1]
    groups = slots // group
    per_step = 4 if groups % 4 == 0 else 1
    width = group * bps * cv
    return pl.pallas_call(
        functools.partial(product_kernel, (cv, bps, group, per_step)),
        grid=(groups // per_step,),
        out_shape=jax.ShapeDtypeStruct((groups, cv, width), jnp.float32),
        in_specs=[
            SMEM,
            pl.BlockSpec((slots, cv, dof), lambda i: (0, 0, 0)),
            pl.BlockSpec((per_step * group, bps, dof, dof), lambda i: (i, 0, 0, 0)),
        ],
        out_specs=pl.BlockSpec((per_step, cv, width), lambda i: (i, 0, 0)),
        scratch_shapes=[
            pltpu.VMEM((slots, cv, dof), jnp.float32),
            pltpu.VMEM((group, LANES, dof), jnp.float32),
        ],
        compiler_params=pltpu.CompilerParams(vmem_limit_bytes=48 << 20),
        name="products",
    )(col_slot, fetched, stiffness)


def fused_kernel(
    dims,
    slot_ref, meta_ref, prolong_ref, stiff_ref,
    meta_out, part_out, scale_out,
    req_ref, stage_ref, fetched_ref, wide_ref, cols_ref, mats_ref, code_ref, factor_ref,
    meta_send, meta_recv, fetch_send, fetch_recv, part_send, part_recv, scale_send, scale_recv,
    mats_sem, own_sem,
):
    gx, gy, cv, bps, group = dims
    n = gx * gy
    me = lax.axis_index("gx") * gy + lax.axis_index("gy")
    barrier = pltpu.get_barrier_semaphore()

    def where(peer):
        return (peer // gy, lax.rem(peer, gy))

    def remote(src, dst, send_sem, recv_sem, peer):
        return pltpu.make_async_remote_copy(
            src_ref=src, dst_ref=dst, send_sem=send_sem, recv_sem=recv_sem,
            device_id=where(peer), device_id_type=MESH,
        )

    def meta_copy(peer, source):
        return remote(
            meta_ref.at[peer], meta_out.at[source], meta_send.at[peer], meta_recv.at[source], peer
        )

    def fetch_copy(peer, source):
        return remote(
            stage_ref.at[pl.ds(peer * group, group)],
            fetched_ref.at[pl.ds(source * group, group)],
            fetch_send.at[peer], fetch_recv.at[source], peer,
        )

    def part_copies(peer, source):
        return (
            remote(code_ref.at[peer], part_out.at[source], part_send.at[peer], part_recv.at[source], peer),
            remote(
                factor_ref.at[peer], scale_out.at[source], scale_send.at[peer], scale_recv.at[source], peer
            ),
        )

    def mats_copy(peer):
        return pltpu.make_async_copy(
            stiff_ref.at[pl.ds(peer * group, group)],
            mats_ref.at[pl.ds(peer * group, group)],
            mats_sem.at[peer],
        )

    def greet(k, c):
        pl.semaphore_signal(barrier, inc=1, device_id=where(lax.rem(me + k, n)), device_id_type=MESH)
        return c

    lax.fori_loop(1, n, greet, 0)
    own_meta = pltpu.make_async_copy(meta_ref.at[me], meta_out.at[me], own_sem.at[0])
    own_meta.start()

    def load(k, c):
        mats_copy(peer_at(k, gx, gy, False)).start()
        return c

    lax.fori_loop(0, n, load, 0)
    pl.semaphore_wait(barrier, n - 1)

    def ask(k, c):
        meta_copy(peer_at(k, gx, gy, True), me).start()
        return c

    lax.fori_loop(0, n - 1, ask, 0)
    own_meta.wait()

    def asked(k, c):
        source = peer_at(k, gx, gy, True)
        meta_copy(source, source).wait()
        return c

    lax.fori_loop(0, n - 1, asked, 0)
    to_scalars = pltpu.make_async_copy(meta_out, req_ref, own_sem.at[1])
    to_scalars.start()
    to_scalars.wait()

    def fill(k, c):
        peer = peer_at(k, gx, gy, True)
        for j in range(group):
            stage_ref[peer * group + j] = prolong_ref[req_ref[peer, 0, j]]
        return c

    lax.fori_loop(0, n, fill, 0)

    def answer(k, c):
        fetch_copy(peer_at(k, gx, gy, True), me).start()
        return c

    lax.fori_loop(0, n - 1, answer, 0)
    for j in range(group):
        wide_ref[me * group + j] = stage_ref[me * group + j].astype(jnp.float32)

    def take(k, c):
        source = peer_at(k, gx, gy, True)
        fetch_copy(source, source).wait()
        for j in range(group):
            wide_ref[source * group + j] = fetched_ref[source * group + j].astype(jnp.float32)
        return c

    lax.fori_loop(0, n - 1, take, 0)
    wide_step = 2 if n % 2 == 0 else 1

    def work(i, c):
        for u in range(wide_step):
            mats_copy(peer_at(i * wide_step + u, gx, gy, False)).wait()
        for u in range(wide_step):
            peer = peer_at(i * wide_step + u, gx, gy, False)
            out = group_product(
                (cv, bps, group), peer, slot_ref, wide_ref, cols_ref.at[u],
                lambda tl: mats_ref[peer * group + tl],
            )
            code_ref[peer], factor_ref[peer] = coded(out)

        @pl.when(i > 0)
        def _():
            for u in range(wide_step):
                for copy in part_copies(peer_at((i - 1) * wide_step + u, gx, gy, False), me):
                    copy.start()

        return c

    lax.fori_loop(0, n // wide_step, work, 0)
    for k in range(n - wide_step, n - 1):
        for copy in part_copies(peer_at(k, gx, gy, False), me):
            copy.start()
    own = (
        pltpu.make_async_copy(code_ref.at[me], part_out.at[me], own_sem.at[2]),
        pltpu.make_async_copy(factor_ref.at[me], scale_out.at[me], own_sem.at[3]),
    )
    for copy in own:
        copy.start()

    def drain(k, c):
        source = peer_at(k, gx, gy, False)
        for copy in part_copies(source, source):
            copy.wait()
        return c

    lax.fori_loop(0, n - 1, drain, 0)
    for copy in own:
        copy.wait()


def fused(meta, prolong, stiffness, col_slot, gx, gy, group):
    slots, bps, dof, _ = stiffness.shape
    cv = prolong.shape[1]
    n = gx * gy
    width = group * bps * cv
    sem = pltpu.SemaphoreType.DMA
    return pl.pallas_call(
        functools.partial(fused_kernel, (gx, gy, cv, bps, group)),
        out_shape=[
            jax.ShapeDtypeStruct(meta.shape, jnp.int32),
            jax.ShapeDtypeStruct((n, cv, width), jnp.int16),
            jax.ShapeDtypeStruct((n, 1, LANES), jnp.float32),
        ],
        in_specs=[SMEM, VMEM, VMEM, HBM],
        out_specs=[VMEM, VMEM, VMEM],
        scratch_shapes=[
            pltpu.SMEM(meta.shape, jnp.int32),
            pltpu.VMEM((slots, cv, dof), jnp.bfloat16),
            pltpu.VMEM((slots, cv, dof), jnp.bfloat16),
            pltpu.VMEM((slots, cv, dof), jnp.float32),
            pltpu.VMEM((2, group, LANES, dof), jnp.float32),
            pltpu.VMEM((slots, bps, dof, dof), jnp.bfloat16),
            pltpu.VMEM((n, cv, width), jnp.int16),
            pltpu.VMEM((n, 1, LANES), jnp.float32),
        ]
        + [sem((n,))] * 9
        + [sem((4,))],
        compiler_params=pltpu.CompilerParams(
            collective_id=1, has_side_effects=True, vmem_limit_bytes=56 << 20
        ),
        name="fused",
    )(col_slot, meta, prolong, stiffness)


def gather_rows_kernel(dims, meta_ref, owner_ref, part_ref, *refs):
    cv, bps, per_peer, group, send_max, quant = dims
    if quant:
        scale_ref, out_ref, out_scale_ref, total_ref, place_ref, seen_ref = refs
    else:
        out_ref, out_scale_ref, total_ref, place_ref, seen_ref = refs
    n = out_ref.shape[0]
    groups, _, width = part_ref.shape
    span = width // group
    total_ref[...] = jnp.zeros_like(total_ref)

    def clear(i, c):
        seen_ref[i] = 0
        return c

    lax.fori_loop(0, n, clear, 0)

    def rank(a, c):
        owner = owner_ref[a]
        before = seen_ref[owner]
        place_ref[a] = owner * send_max + before
        seen_ref[owner] = before + 1
        return c

    lax.fori_loop(0, owner_ref.shape[0], rank, 0)
    lane = lax.broadcasted_iota(jnp.int32, (cv, width), 1)
    column = lax.broadcasted_iota(jnp.int32, (width, width), 0)
    row_lane = lax.broadcasted_iota(jnp.int32, (1, width), 1)

    def body(g, c):
        at = row_lane
        for j in range(group * bps):
            t = g * group + j // bps
            pos = meta_ref[t // per_peer, 0, per_peer + (t % per_peer) * bps + j % bps]
            at = at + jnp.where(row_lane // cv == j, cv * (pos - j), 0)
        hot = jnp.where(column == at, 1.0, 0.0).astype(jnp.bfloat16)
        if quant:
            code = part_ref[g].astype(jnp.int32)
            high = code >> 8
            pieces = [high.astype(jnp.float32), (code - high * 256).astype(jnp.float32)]
            weights = [256.0, 1.0]
        else:
            rest = part_ref[g]
            pieces, weights = [], [1.0, 1.0, 1.0]
            for _ in range(3):
                piece = rest.astype(jnp.bfloat16).astype(jnp.float32)
                pieces.append(piece)
                rest = rest - piece
        placed = 0.0
        for piece, weight in zip(pieces, weights):
            stack = jnp.concatenate(
                [
                    jnp.where((lane >= span * tl) & (lane < span * (tl + 1)), piece, 0.0)
                    for tl in range(group)
                ],
                axis=0,
            ).astype(jnp.bfloat16)
            placed = placed + weight * lax.dot_general(
                stack, hot, NT, preferred_element_type=jnp.float32
            )
        if quant:
            factor = as_column(scale_ref[g], cv)
        for tl in range(group):
            t = g * group + tl
            where = place_ref[meta_ref[t // per_peer, 0, t % per_peer]]
            rows = placed[tl * cv : (tl + 1) * cv]
            if quant:
                rows = rows * factor
            total_ref[where] = total_ref[where] + rows
        return c

    lax.fori_loop(0, groups, body, 0, unroll=4)

    def emit(p, c):
        rows = total_ref[pl.ds(p * send_max, send_max)].reshape(send_max * cv, width)
        out_ref[p], out_scale_ref[p] = coded(rows)
        return c

    lax.fori_loop(0, n, emit, 0, unroll=4)


def gathered_rows(part, scale, meta, owners, n, send_max, group, bps, per_peer):
    groups, cv, width = part.shape
    quant = scale is not None
    args = [meta, owners, part] + ([scale] if quant else [])
    return pl.pallas_call(
        functools.partial(gather_rows_kernel, (cv, bps, per_peer, group, send_max, quant)),
        out_shape=[
            jax.ShapeDtypeStruct((n, send_max * cv, width), jnp.int16),
            jax.ShapeDtypeStruct((n, 1, LANES), jnp.float32),
        ],
        in_specs=[SMEM, SMEM] + [VMEM] * (len(args) - 2),
        out_specs=[VMEM, VMEM],
        scratch_shapes=[
            pltpu.VMEM((n * send_max, cv, width), jnp.float32),
            pltpu.SMEM((owners.shape[0],), jnp.int32),
            pltpu.SMEM((n,), jnp.int32),
        ],
        compiler_params=pltpu.CompilerParams(vmem_limit_bytes=48 << 20),
        name="gathered_rows",
    )(*args)


def per_device(gx, gy, prolong, stiffness, request, col_slot, col_pos, coarse_owner):
    n = gx * gy
    own_aggs, cv, dof = prolong.shape
    slots, bps = col_slot.shape
    per_peer = slots // n
    group = MAXNB // bps
    quant = per_peer == group
    send_max = (2 * own_aggs + n - 1) // n

    meta = jnp.concatenate([request.reshape(n, per_peer), col_pos.reshape(n, per_peer * bps)], axis=1)
    meta = jnp.pad(meta, ((0, 0), (0, LANES - meta.shape[1])))[:, None, :]
    if quant:
        meta_in, part, scale = fused(meta, prolong, stiffness, col_slot, gx, gy, group)
    else:
        (meta_in,) = exchange([meta], gx, gy, 1)
        answer = prolong[meta_in[:, 0, :per_peer].reshape(-1)].reshape(n, per_peer * cv, dof)
        (fetched,) = exchange([answer], gx, gy, 2)
        made = products(fetched.reshape(slots, cv, dof), stiffness, col_slot, group)
        flat = made.reshape(slots // group, cv, group, bps * cv).transpose(0, 2, 1, 3)
        (flat,) = exchange([flat.reshape(n, per_peer * cv, bps * cv)], gx, gy, 3)
        flat = flat.reshape(slots // group, group, cv, bps * cv).transpose(0, 2, 1, 3)
        part, scale = flat.reshape(slots // group, cv, group * bps * cv), None
    code, factor = gathered_rows(
        part, scale, meta_in, coarse_owner[:, 0], n, send_max, group, bps, per_peer
    )
    return delivered(code, factor, cv, gx, gy)


def solution(mesh):
    gx, gy = mesh.shape["gx"], mesh.shape["gy"]
    placed = (
        P(AXES, None, None),
        P(AXES, None, None, None),
        P(AXES),
        P(AXES, None),
        P(AXES, None),
        P(AXES, None),
    )
    return jax.shard_map(
        functools.partial(per_device, gx, gy),
        mesh=mesh,
        in_specs=placed,
        out_specs=P(AXES, None, None),
        check_vma=False,
    )
```

profile of v0, /device:TPU:11, one launch (start us, length us, event | category | flops | bytes accessed | tf_op | source)
XLA Modules:
  0.0 137.6 jit_solution(18051525778887870192)
XLA Ops:
  0.0 0.7 reshape.6
  0.8 1.4 %copy.10.slot_ref = s32[128,4]{1,0:T(8,128)} copy(s32[128,4]{0,1:T(4,128)} %param.9) | data formatting | bytes 4096 | tf_op args[3]
  2.2 0.8 copy.9
  3.0 0.1 reshape.7
  3.0 0.1 pad_add_fusion
  3.1 0.6 pad.4
  3.7 0.0 copy-start.3
  3.7 53.3 %fused.1 = (s32[32,1,128]{2,1,0:T(1,128)}, s16[32,24,384]{2,1,0:T(8,128)(2,1)}, f32[32,1,128]{2,1,0:T(1,128)}) custom-call(s32[128,4]{1,0:T(8,128)} %copy.10.slot_ref, s32[32,1,128]{2,1,0:T(1,128)} %bitcast.3, bf16[64,24,128]{2,1,0:T(8,128)(2,1)} %prolong_ref.1, bf16[128,4,128,128]{3,2,1,0:T(8,128)(2,1)} %stiff_ref.1), custom_call_target="tpu_custom_call" | custom-call | tf_op jit(solution)/shard_map/fused/pallas_call | solution.py:454
  57.1 0.0 copy-done.3
  57.1 0.0 copy-start
  57.1 1.1 copy-done
  58.1 0.0 copy-start.1
  58.1 0.7 copy-done.1
  58.9 0.0 copy-start.2
  58.9 0.7 copy-done.2
  59.6 11.2 %gathered_rows.1 = (s16[32,96,384]{2,1,0:T(8,128)(2,1)S(1)}, f32[32,1,128]{2,1,0:T(1,128)S(1)}) custom-call(s32[32,1,128]{2,1,0:T(1,128)S(1)} %copy-done.1, s32[64]{0:T(128)S(1)} %bitcast.2, s16[32,24,384]{2,1,0:T(8,128)(2,1)S(1)} %copy-done, f32[32,1,128]{2,1,0:T(1,128)S(1)} %copy-done.2), custom_call_target="tpu_custom_call" | custom-call | tf_op jit(solution)/shard_map/gathered_rows/pallas_call | solution.py:567
  70.8 64.6 %delivered.1 = f32[128,24,384]{2,1,0:T(8,128)S(1)} custom-call(s16[32,96,384]{2,1,0:T(8,128)(2,1)S(1)} %get-tuple-element.13.code_ref, f32[32,1,128]{2,1,0:T(1,128)S(1)} %get-tuple-element.14.scale_ref), custom_call_target="tpu_custom_call" | custom-call | tf_op jit(solution)/shard_map/delivered/pallas_call | solution.py:109
  135.4 2.2 %copy.12 = f32[128,24,384]{2,1,0:T(8,128)} copy(f32[128,24,384]{2,1,0:T(8,128)S(1)} %delivered.1) | data formatting | bytes 9437184
Async XLA Ops:
  3.7 53.3 %copy-start.3 = (s32[64,1]{0,1:T(1,128)S(1)}, s32[64,1]{0,1:T(1,128)}, u32[]{:S(2)}) copy-start(s32[64,1]{0,1:T(1,128)} %param.11) | copy-start | bytes 772
  57.1 1.1 copy-start
  58.1 0.7 copy-start.1
  58.9 0.7 copy-start.2
where the time goes:
time: 138 us
  Pallas kernels  129 us (93%)
  local copies, waits for them, and re-layouts  8.33 us (6%)
    pallas_call x1, Pallas kernels, delivered(): pl.pallas_call(functools.partial(deliver_kernel, (gx, gy, cv)), out_shape...  64.6 us
    pallas_call x1, Pallas kernels, fused(): pl.pallas_call(functools.partial(fused_kernel, (gx, gy, cv, bps, group)),...  53.3 us
    pallas_call x1, Pallas kernels, gathered_rows(): pl.pallas_call(functools.partial(gather_rows_kernel, (cv, bps, per_peer,...  11.2 us
    unnamed x11, local copies, waits for them, and re-layouts  6.89 us

commit v1 on v0

--- a/solution.py
+++ b/solution.py
@@ -297,17 +297,67 @@
     )(col_slot, fetched, stiffness)
 
 
+def offset_at(i, side, sign, gx, gy):
+    half = gx // 2
+    x, y = lax.axis_index("gx"), lax.axis_index("gy")
+    row = lax.rem(lax.rem(x, half) + sign * (i // gy) + half, half)
+    col = lax.rem(y + sign * lax.rem(i, gy) + gy, gy)
+    return (side * half + row) * gy + col
+
+
+def mixed_at(k, sign, gx, gy):
+    count = gx // 2 * gy
+    near = lax.rem(k, 2)
+    side = lax.rem(lax.axis_index("gx") // (gx // 2) + 1 + near, 2)
+    return offset_at(lax.rem(k // 2 + near, count), side, sign, gx, gy)
+
+
+def group_tail(dims, grp, slot_ref, wide_ref, cols_ref, proj_ref):
+    cv, bps, group = dims
+    span = bps * cv
+    lane = lax.broadcasted_iota(jnp.int32, (cv, LANES), 1)
+    for tl in range(group):
+        for q in range(bps):
+            block = wide_ref[slot_ref[q, grp * group + tl]]
+            at = (span * tl + cv * q) % LANES
+            first = min(cv, LANES - at)
+            cols_ref[tl, at : at + first, :] = block[:first]
+            if first < cv:
+                cols_ref[tl, 0 : cv - first, :] = block[first:]
+    ends = []
+    for tl in range(group):
+        cols = cols_ref[tl].astype(jnp.bfloat16)
+        prod = lax.dot_general(proj_ref[grp * group + tl], cols, NT, preferred_element_type=jnp.float32)
+        both = prod[:span] + prod[span:]
+        rel = (lane + (LANES * tl - span * tl) % LANES) % LANES
+        one = both[(bps - 1) * cv :]
+        for q in range(bps - 2, -1, -1):
+            one = jnp.where(rel < cv * (q + 1), both[q * cv : (q + 1) * cv], one)
+        ends.append(one)
+    tiles = []
+    for j in range(span * group // LANES):
+        low, high = LANES * j // span, (LANES * (j + 1) - 1) // span
+        tile = ends[high]
+        for tl in range(high - 1, low - 1, -1):
+            tile = jnp.where(lane < span * (tl + 1) - LANES * j, ends[tl], tile)
+        tiles.append(tile)
+    return jnp.concatenate(tiles, axis=1)
+
+
 def fused_kernel(
     dims,
     slot_ref, meta_ref, prolong_ref, stiff_ref,
     meta_out, part_out, scale_out,
-    req_ref, stage_ref, fetched_ref, wide_ref, cols_ref, mats_ref, code_ref, factor_ref,
+    meta_land, req_ref, stage_ref, fetched_ref, wide_ref, cols_ref, mats_ref, proj_ref, code_ref, factor_ref,
     meta_send, meta_recv, fetch_send, fetch_recv, part_send, part_recv, scale_send, scale_recv,
     mats_sem, own_sem,
 ):
     gx, gy, cv, bps, group = dims
     n = gx * gy
+    count = n // 2
+    span = bps * cv
     me = lax.axis_index("gx") * gy + lax.axis_index("gy")
+    side = lax.axis_index("gx") // (gx // 2)
     barrier = pltpu.get_barrier_semaphore()
 
     def where(peer):
@@ -321,7 +371,8 @@
 
     def meta_copy(peer, source):
         return remote(
-            meta_ref.at[peer], meta_out.at[source], meta_send.at[peer], meta_recv.at[source], peer
+            meta_ref.at[lax.rem(peer, count)], meta_land.at[source],
+            meta_send.at[peer], meta_recv.at[source], peer,
         )
 
     def fetch_copy(peer, source):
@@ -332,11 +383,10 @@
         )
 
     def part_copies(peer, source):
+        at = lax.rem(peer, count)
         return (
-            remote(code_ref.at[peer], part_out.at[source], part_send.at[peer], part_recv.at[source], peer),
-            remote(
-                factor_ref.at[peer], scale_out.at[source], scale_send.at[peer], scale_recv.at[source], peer
-            ),
+            remote(factor_ref.at[at], scale_out.at[source], scale_send.at[peer], scale_recv.at[source], peer),
+            remote(code_ref.at[at], part_out.at[source], part_send.at[peer], part_recv.at[source], peer),
         )
 
     def mats_copy(peer):
@@ -351,91 +401,113 @@
         return c
 
     lax.fori_loop(1, n, greet, 0)
-    own_meta = pltpu.make_async_copy(meta_ref.at[me], meta_out.at[me], own_sem.at[0])
+    own_meta = pltpu.make_async_copy(meta_ref.at[lax.rem(me, count)], meta_land.at[me], own_sem.at[0])
     own_meta.start()
+    mats_copy(me).start()
 
     def load(k, c):
-        mats_copy(peer_at(k, gx, gy, False)).start()
-        return c
-
-    lax.fori_loop(0, n, load, 0)
+        mats_copy(mixed_at(k, -1, gx, gy)).start()
+        return c
+
+    lax.fori_loop(0, n - 1, load, 0)
     pl.semaphore_wait(barrier, n - 1)
 
     def ask(k, c):
-        meta_copy(peer_at(k, gx, gy, True), me).start()
+        meta_copy(mixed_at(k, 1, gx, gy), me).start()
         return c
 
     lax.fori_loop(0, n - 1, ask, 0)
     own_meta.wait()
 
     def asked(k, c):
-        source = peer_at(k, gx, gy, True)
+        source = mixed_at(k, -1, gx, gy)
         meta_copy(source, source).wait()
         return c
 
     lax.fori_loop(0, n - 1, asked, 0)
-    to_scalars = pltpu.make_async_copy(meta_out, req_ref, own_sem.at[1])
+    to_scalars = pltpu.make_async_copy(meta_land, req_ref, own_sem.at[1])
     to_scalars.start()
+    to_next = pltpu.make_async_copy(meta_land, meta_out, own_sem.at[2])
+    to_next.start()
     to_scalars.wait()
+    first = side * (group + group * bps)
 
     def fill(k, c):
-        peer = peer_at(k, gx, gy, True)
+        peer = mixed_at(k, 1, gx, gy)
         for j in range(group):
-            stage_ref[peer * group + j] = prolong_ref[req_ref[peer, 0, j]]
-        return c
-
-    lax.fori_loop(0, n, fill, 0)
+            stage_ref[peer * group + j] = prolong_ref[req_ref[peer, 0, first + j]]
+        return c
+
+    lax.fori_loop(0, n - 1, fill, 0)
+    for j in range(group):
+        stage_ref[me * group + j] = prolong_ref[req_ref[me, 0, first + j]]
 
     def answer(k, c):
-        fetch_copy(peer_at(k, gx, gy, True), me).start()
+        fetch_copy(mixed_at(k, 1, gx, gy), me).start()
         return c
 
     lax.fori_loop(0, n - 1, answer, 0)
-    for j in range(group):
-        wide_ref[me * group + j] = stage_ref[me * group + j].astype(jnp.float32)
+
+    def project(source, from_ref):
+        mats_copy(source).wait()
+        for j in range(group):
+            t = source * group + j
+            block = from_ref[t]
+            wide_ref[t] = block.astype(jnp.float32)
+            mats = mats_ref[t]
+            mats = jnp.concatenate([mats[q] for q in range(bps)], axis=1)
+            prod = jnp.dot(block, mats, preferred_element_type=jnp.float32)
+            rows = jnp.concatenate([prod[:, q * LANES : (q + 1) * LANES] for q in range(bps)], axis=0)
+            hi = rows.astype(jnp.bfloat16)
+            proj_ref[t, 0:span] = hi
+            proj_ref[t, span : 2 * span] = (rows - hi.astype(jnp.float32)).astype(jnp.bfloat16)
+
+    project(me, stage_ref)
 
     def take(k, c):
-        source = peer_at(k, gx, gy, True)
-        fetch_copy(source, source).wait()
-        for j in range(group):
-            wide_ref[source * group + j] = fetched_ref[source * group + j].astype(jnp.float32)
+        source = mixed_at(k, -1, gx, gy)
+        fetch_copy(source, source).wait_recv()
+        project(source, fetched_ref)
         return c
 
     lax.fori_loop(0, n - 1, take, 0)
-    wide_step = 2 if n % 2 == 0 else 1
-
-    def work(i, c):
-        for u in range(wide_step):
-            mats_copy(peer_at(i * wide_step + u, gx, gy, False)).wait()
-        for u in range(wide_step):
-            peer = peer_at(i * wide_step + u, gx, gy, False)
-            out = group_product(
-                (cv, bps, group), peer, slot_ref, wide_ref, cols_ref.at[u],
-                lambda tl: mats_ref[peer * group + tl],
+
+    def send(j, both):
+        i = lax.rem(j + 1, count)
+        for copy in part_copies(offset_at(i, 1 - side, 1, gx, gy), me):
+            copy.start()
+        if both:
+            for copy in part_copies(offset_at(i, side, 1, gx, gy), me):
+                copy.start()
+
+    def work(j, c):
+        at = lax.rem(offset_at(lax.rem(j + 1, count), side, 1, gx, gy), count)
+        for u in range(2):
+            out = group_tail(
+                (cv, bps, group), u * count + at, slot_ref, wide_ref, cols_ref.at[u], proj_ref
             )
-            code_ref[peer], factor_ref[peer] = coded(out)
-
-        @pl.when(i > 0)
+            code_ref[at, u], factor_ref[at, u] = coded(out)
+
+        @pl.when(j > 0)
         def _():
-            for u in range(wide_step):
-                for copy in part_copies(peer_at((i - 1) * wide_step + u, gx, gy, False), me):
-                    copy.start()
-
-        return c
-
-    lax.fori_loop(0, n // wide_step, work, 0)
-    for k in range(n - wide_step, n - 1):
-        for copy in part_copies(peer_at(k, gx, gy, False), me):
-            copy.start()
+            send(j - 1, True)
+
+        return c
+
+    lax.fori_loop(0, count, work, 0)
+    send(count - 1, False)
+    mine = lax.rem(me, count)
     own = (
-        pltpu.make_async_copy(code_ref.at[me], part_out.at[me], own_sem.at[2]),
-        pltpu.make_async_copy(factor_ref.at[me], scale_out.at[me], own_sem.at[3]),
+        pltpu.make_async_copy(code_ref.at[mine], part_out.at[me], own_sem.at[3]),
+        pltpu.make_async_copy(factor_ref.at[mine], scale_out.at[me], own_sem.at[4]),
     )
     for copy in own:
         copy.start()
+    to_next.wait()
 
     def drain(k, c):
-        source = peer_at(k, gx, gy, False)
+        source = mixed_at(k, -1, gx, gy)
+        fetch_copy(source, source).wait_send()
         for copy in part_copies(source, source):
             copy.wait()
         return c
@@ -449,42 +521,269 @@
     slots, bps, dof, _ = stiffness.shape
     cv = prolong.shape[1]
     n = gx * gy
+    count = n // 2
     width = group * bps * cv
     sem = pltpu.SemaphoreType.DMA
     return pl.pallas_call(
         functools.partial(fused_kernel, (gx, gy, cv, bps, group)),
         out_shape=[
-            jax.ShapeDtypeStruct(meta.shape, jnp.int32),
-            jax.ShapeDtypeStruct((n, cv, width), jnp.int16),
-            jax.ShapeDtypeStruct((n, 1, LANES), jnp.float32),
+            jax.ShapeDtypeStruct((n, 1, LANES), jnp.int32),
+            jax.ShapeDtypeStruct((n, 2, cv, width), jnp.int16),
+            jax.ShapeDtypeStruct((n, 2, 1, LANES), jnp.float32),
         ],
         in_specs=[SMEM, VMEM, VMEM, HBM],
-        out_specs=[VMEM, VMEM, VMEM],
+        out_specs=[HBM, HBM, HBM],
         scratch_shapes=[
-            pltpu.SMEM(meta.shape, jnp.int32),
+            pltpu.VMEM((n, 1, LANES), jnp.int32),
+            pltpu.SMEM((n, 1, LANES), jnp.int32),
             pltpu.VMEM((slots, cv, dof), jnp.bfloat16),
             pltpu.VMEM((slots, cv, dof), jnp.bfloat16),
             pltpu.VMEM((slots, cv, dof), jnp.float32),
             pltpu.VMEM((2, group, LANES, dof), jnp.float32),
             pltpu.VMEM((slots, bps, dof, dof), jnp.bfloat16),
-            pltpu.VMEM((n, cv, width), jnp.int16),
-            pltpu.VMEM((n, 1, LANES), jnp.float32),
+            pltpu.VMEM((slots, 2 * bps * cv, dof), jnp.bfloat16),
+            pltpu.VMEM((count, 2, cv, width), jnp.int16),
+            pltpu.VMEM((count, 2, 1, LANES), jnp.float32),
         ]
         + [sem((n,))] * 9
-        + [sem((4,))],
+        + [sem((5,))],
         compiler_params=pltpu.CompilerParams(
-            collective_id=1, has_side_effects=True, vmem_limit_bytes=56 << 20
+            collective_id=1, has_side_effects=True, vmem_limit_bytes=40 << 20
         ),
         name="fused",
     )(col_slot, meta, prolong, stiffness)
 
 
+def collect_kernel(dims, meta_ref, part_ref, scale_ref, total_ref, place_ref, seen_ref, item_ref, slot_ref):
+    gx, gy, cv, bps, group, send_max, own_aggs, unroll = dims
+    n = gx * gy
+    count = n // 2
+    span = bps * cv
+    width = group * span
+    trash = n * send_max
+    me = lax.axis_index("gx") * gy + lax.axis_index("gy")
+    side, mine = me // count, lax.rem(me, count)
+    each = group + group * bps
+    total_ref[...] = jnp.zeros_like(total_ref)
+
+    def clear(i, c):
+        seen_ref[i] = 0
+        return c
+
+    lax.fori_loop(0, 2 * n, clear, 0)
+
+    def rank(a, c):
+        for kk in range(2):
+            owner = meta_ref[kk * count + mine, 0, 2 * each + a]
+            before = seen_ref[kk * n + owner]
+            seen_ref[kk * n + owner] = before + 1
+            at = (lax.rem(owner, count) * 2 + kk) * send_max + before
+            place_ref[kk * own_aggs + a] = jnp.where(owner // count == side, at, -1)
+        return c
+
+    lax.fori_loop(0, own_aggs, rank, 0, unroll=4)
+
+    def listed(d, used):
+        for kk in range(2):
+            for tl in range(group):
+                at = place_ref[kk * own_aggs + meta_ref[d, 0, kk * each + tl]]
+                item_ref[used] = (d * 2 + kk) * group + tl
+                slot_ref[used] = at
+                used = used + jnp.where(at >= 0, 1, 0)
+        return used
+
+    used = lax.fori_loop(0, n, listed, 0, unroll=2)
+    for u in range(unroll):
+        item_ref[used + u] = 0
+        slot_ref[used + u] = trash
+    lane = lax.broadcasted_iota(jnp.int32, (cv, LANES), 1)
+    ahead = lax.broadcasted_iota(jnp.int32, (cv, width), 1) - lax.broadcasted_iota(jnp.int32, (cv, width), 0)
+    rest = jnp.zeros((LANES - span, width), jnp.float32)
+
+    def body(g, c):
+        for u in range(unroll):
+            item = item_ref[g * unroll + u]
+            slot = slot_ref[g * unroll + u]
+            d, kk, tl = item // (2 * group), lax.rem(item // group, 2), lax.rem(item, group)
+            begin = span * tl
+            low, high = begin // LANES, (begin + span - 1) // LANES
+            x0 = part_ref[d, kk, :, pl.ds(pl.multiple_of(low * LANES, LANES), LANES)].astype(jnp.int32)
+            x1 = part_ref[d, kk, :, pl.ds(pl.multiple_of(high * LANES, LANES), LANES)].astype(jnp.int32)
+            x = jnp.where(lane >= lax.rem(begin, LANES), x0, x1)
+            x = pltpu.roll(x, lax.rem((LANES - span) * tl, LANES), 1)
+            top = x >> 8
+            stack = jnp.concatenate([top.astype(jnp.float32), (x - top * 256).astype(jnp.float32)], axis=0)
+            hot = jnp.concatenate(
+                [
+                    jnp.where(ahead == cv * meta_ref[d, 0, kk * each + group + tl * bps + q], 1.0, 0.0)
+                    for q in range(bps)
+                ]
+                + [rest],
+                axis=0,
+            )
+            placed = jnp.dot(
+                stack.astype(jnp.bfloat16), hot.astype(jnp.bfloat16), preferred_element_type=jnp.float32
+            )
+            rows = (placed[:cv] * 256.0 + placed[cv:]) * as_column(scale_ref[d, kk], cv)
+            total_ref[slot] = total_ref[slot] + rows
+        return c
+
+    lax.fori_loop(0, (used + unroll - 1) // unroll, body, 0)
+
+
+def collected(part, scale, meta, gx, gy, send_max, group, bps, own_aggs):
+    n, _, cv, width = part.shape
+    unroll = 4
+    most = n * 2 * group + unroll
+    return pl.pallas_call(
+        functools.partial(collect_kernel, (gx, gy, cv, bps, group, send_max, own_aggs, unroll)),
+        out_shape=jax.ShapeDtypeStruct((n * send_max + 1, cv, width), jnp.float32),
+        in_specs=[SMEM, VMEM, VMEM],
+        out_specs=VMEM,
+        scratch_shapes=[
+            pltpu.SMEM((2 * own_aggs,), jnp.int32),
+            pltpu.SMEM((2 * n,), jnp.int32),
+            pltpu.SMEM((most,), jnp.int32),
+            pltpu.SMEM((most,), jnp.int32),
+        ],
+        compiler_params=pltpu.CompilerParams(vmem_limit_bytes=24 << 20),
+        name="collected",
+    )(meta, part, scale)
+
+
+def handed_kernel(
+    dims, total_ref, out_ref,
+    code_ref, scale_ref, land_ref, land_scale, wide_ref,
+    code_send, code_recv, scale_send, scale_recv, out_sem,
+):
+    gx, gy, send_max = dims
+    n = gx * gy
+    count = n // 2
+    cv, width = total_ref.shape[1:]
+    rows = send_max * cv
+    me = lax.axis_index("gx") * gy + lax.axis_index("gy")
+    side, mine = me // count, lax.rem(me, count)
+    barrier = pltpu.get_barrier_semaphore()
+
+    def where(at):
+        peer = side * count + at
+        return (peer // gy, lax.rem(peer, gy))
+
+    def at_offset(i, sign):
+        return lax.rem(offset_at(i, side, sign, gx, gy), count)
+
+    def greet(k, c):
+        pl.semaphore_signal(barrier, inc=1, device_id=where(at_offset(k, 1)), device_id_type=MESH)
+        return c
+
+    lax.fori_loop(1, count, greet, 0)
+
+    def copies(peer, source):
+        return [
+            pltpu.make_async_remote_copy(
+                src_ref=src.at[peer], dst_ref=dst.at[source],
+                send_sem=send.at[peer], recv_sem=recv.at[source],
+                device_id=where(peer), device_id_type=MESH,
+            )
+            for src, dst, send, recv in (
+                (scale_ref, land_scale, scale_send, scale_recv),
+                (code_ref, land_ref, code_send, code_recv),
+            )
+        ]
+
+    def out_copy(p):
+        at = pl.ds(p * send_max, send_max)
+        return pltpu.make_async_copy(wide_ref.at[at], out_ref.at[at], out_sem.at[p])
+
+    def own_copy(kk):
+        return pltpu.make_async_copy(
+            total_ref.at[pl.ds((mine * 2 + kk) * send_max, send_max)],
+            out_ref.at[pl.ds((kk * count + mine) * send_max, send_max)],
+            out_sem.at[kk * count + mine],
+        )
+
+    for kk in range(2):
+        own_copy(kk).start()
+
+    def code(i):
+        at = at_offset(i, 1)
+        for kk in range(2):
+            values = total_ref[pl.ds((at * 2 + kk) * send_max, send_max)].reshape(rows, width)
+            code_ref[at, kk], scale_ref[at, kk] = coded(values)
+
+    def send(i):
+        for copy in copies(at_offset(i, 1), mine):
+            copy.start()
+
+    code(1)
+    pl.semaphore_wait(barrier, count - 1)
+
+    def work(i, c):
+        code(i)
+        send(i - 1)
+        return c
+
+    lax.fori_loop(2, count, work, 0)
+    send(count - 1)
+
+    def drain(i, c):
+        source = at_offset(i, -1)
+        for copy in copies(source, source):
+            copy.wait_recv()
+        for kk in range(2):
+            values = land_ref[source, kk].astype(jnp.int32).astype(jnp.float32)
+            values = values * as_column(land_scale[source, kk], rows)
+            p = kk * count + source
+            wide_ref[pl.ds(p * send_max, send_max)] = values.reshape(send_max, cv, width)
+            out_copy(p).start()
+        return c
+
+    lax.fori_loop(1, count, drain, 0)
+
+    def finish(i, c):
+        for copy in copies(at_offset(i, 1), mine):
+            copy.wait_send()
+        for kk in range(2):
+            out_copy(kk * count + at_offset(i, 1)).wait()
+        return c
+
+    lax.fori_loop(1, count, finish, 0)
+    for kk in range(2):
+        own_copy(kk).wait()
+
+
+def handed(total, send_max, gx, gy):
+    n = gx * gy
+    count = n // 2
+    _, cv, width = total.shape
+    sem = pltpu.SemaphoreType.DMA
+    out = (n * send_max, cv, width)
+    codes = (count, 2, send_max * cv, width)
+    scales = (count, 2, 1, LANES)
+    return pl.pallas_call(
+        functools.partial(handed_kernel, (gx, gy, send_max)),
+        out_shape=jax.ShapeDtypeStruct(out, jnp.float32),
+        in_specs=[VMEM],
+        out_specs=HBM,
+        scratch_shapes=[
+            pltpu.VMEM(codes, jnp.int16),
+            pltpu.VMEM(scales, jnp.float32),
+            pltpu.VMEM(codes, jnp.int16),
+            pltpu.VMEM(scales, jnp.float32),
+            pltpu.VMEM(out, jnp.float32),
+        ]
+        + [sem((count,))] * 4
+        + [sem((n,))],
+        compiler_params=pltpu.CompilerParams(
+            collective_id=5, has_side_effects=True, vmem_limit_bytes=40 << 20
+        ),
+        name="handed",
+    )(total)
+
+
 def gather_rows_kernel(dims, meta_ref, owner_ref, part_ref, *refs):
-    cv, bps, per_peer, group, send_max, quant = dims
-    if quant:
-        scale_ref, out_ref, out_scale_ref, total_ref, place_ref, seen_ref = refs
-    else:
-        out_ref, out_scale_ref, total_ref, place_ref, seen_ref = refs
+    cv, bps, per_peer, group, send_max = dims
+    out_ref, out_scale_ref, total_ref, place_ref, seen_ref = refs
     n = out_ref.shape[0]
     groups, _, width = part_ref.shape
     span = width // group
@@ -515,20 +814,14 @@
             pos = meta_ref[t // per_peer, 0, per_peer + (t % per_peer) * bps + j % bps]
             at = at + jnp.where(row_lane // cv == j, cv * (pos - j), 0)
         hot = jnp.where(column == at, 1.0, 0.0).astype(jnp.bfloat16)
-        if quant:
-            code = part_ref[g].astype(jnp.int32)
-            high = code >> 8
-            pieces = [high.astype(jnp.float32), (code - high * 256).astype(jnp.float32)]
-            weights = [256.0, 1.0]
-        else:
-            rest = part_ref[g]
-            pieces, weights = [], [1.0, 1.0, 1.0]
-            for _ in range(3):
-                piece = rest.astype(jnp.bfloat16).astype(jnp.float32)
-                pieces.append(piece)
-                rest = rest - piece
+        rest = part_ref[g]
+        pieces = []
+        for _ in range(3):
+            piece = rest.astype(jnp.bfloat16).astype(jnp.float32)
+            pieces.append(piece)
+            rest = rest - piece
         placed = 0.0
-        for piece, weight in zip(pieces, weights):
+        for piece in pieces:
             stack = jnp.concatenate(
                 [
                     jnp.where((lane >= span * tl) & (lane < span * (tl + 1)), piece, 0.0)
@@ -536,17 +829,13 @@
                 ],
                 axis=0,
             ).astype(jnp.bfloat16)
-            placed = placed + weight * lax.dot_general(
+            placed = placed + lax.dot_general(
                 stack, hot, NT, preferred_element_type=jnp.float32
             )
-        if quant:
-            factor = as_column(scale_ref[g], cv)
         for tl in range(group):
             t = g * group + tl
             where = place_ref[meta_ref[t // per_peer, 0, t % per_peer]]
             rows = placed[tl * cv : (tl + 1) * cv]
-            if quant:
-                rows = rows * factor
             total_ref[where] = total_ref[where] + rows
         return c
 
@@ -560,17 +849,15 @@
     lax.fori_loop(0, n, emit, 0, unroll=4)
 
 
-def gathered_rows(part, scale, meta, owners, n, send_max, group, bps, per_peer):
+def gathered_rows(part, meta, owners, n, send_max, group, bps, per_peer):
     groups, cv, width = part.shape
-    quant = scale is not None
-    args = [meta, owners, part] + ([scale] if quant else [])
     return pl.pallas_call(
-        functools.partial(gather_rows_kernel, (cv, bps, per_peer, group, send_max, quant)),
+        functools.partial(gather_rows_kernel, (cv, bps, per_peer, group, send_max)),
         out_shape=[
             jax.ShapeDtypeStruct((n, send_max * cv, width), jnp.int16),
             jax.ShapeDtypeStruct((n, 1, LANES), jnp.float32),
         ],
-        in_specs=[SMEM, SMEM] + [VMEM] * (len(args) - 2),
+        in_specs=[SMEM, SMEM, VMEM],
         out_specs=[VMEM, VMEM],
         scratch_shapes=[
             pltpu.VMEM((n * send_max, cv, width), jnp.float32),
@@ -579,7 +866,7 @@
         ],
         compiler_params=pltpu.CompilerParams(vmem_limit_bytes=48 << 20),
         name="gathered_rows",
-    )(*args)
+    )(meta, owners, part)
 
 
 def per_device(gx, gy, prolong, stiffness, request, col_slot, col_pos, coarse_owner):
@@ -588,25 +875,29 @@
     slots, bps = col_slot.shape
     per_peer = slots // n
     group = MAXNB // bps
-    quant = per_peer == group
     send_max = (2 * own_aggs + n - 1) // n
-
-    meta = jnp.concatenate([request.reshape(n, per_peer), col_pos.reshape(n, per_peer * bps)], axis=1)
-    meta = jnp.pad(meta, ((0, 0), (0, LANES - meta.shape[1])))[:, None, :]
-    if quant:
-        meta_in, part, scale = fused(meta, prolong, stiffness, col_slot, gx, gy, group)
-    else:
-        (meta_in,) = exchange([meta], gx, gy, 1)
-        answer = prolong[meta_in[:, 0, :per_peer].reshape(-1)].reshape(n, per_peer * cv, dof)
-        (fetched,) = exchange([answer], gx, gy, 2)
-        made = products(fetched.reshape(slots, cv, dof), stiffness, col_slot, group)
-        flat = made.reshape(slots // group, cv, group, bps * cv).transpose(0, 2, 1, 3)
-        (flat,) = exchange([flat.reshape(n, per_peer * cv, bps * cv)], gx, gy, 3)
-        flat = flat.reshape(slots // group, group, cv, bps * cv).transpose(0, 2, 1, 3)
-        part, scale = flat.reshape(slots // group, cv, group * bps * cv), None
-    code, factor = gathered_rows(
-        part, scale, meta_in, coarse_owner[:, 0], n, send_max, group, bps, per_peer
-    )
+    each = per_peer + per_peer * bps
+    halved = per_peer == group and gx % 2 == 0 and 2 * each + own_aggs <= LANES
+
+    parts = jnp.concatenate([request.reshape(n, per_peer), col_pos.reshape(n, per_peer * bps)], axis=1)
+    if halved:
+        count = n // 2
+        owners = jnp.broadcast_to(coarse_owner[:, 0], (count, own_aggs))
+        meta = jnp.concatenate([parts[:count], parts[count:], owners], axis=1)
+        meta = jnp.pad(meta, ((0, 0), (0, LANES - meta.shape[1])))[:, None, :]
+        meta_in, part, scale = fused(meta, prolong, stiffness, col_slot.T, gx, gy, group)
+        total = collected(part, scale, meta_in, gx, gy, send_max, group, bps, own_aggs)
+        return handed(total, send_max, gx, gy)
+    meta = jnp.pad(parts, ((0, 0), (0, LANES - each)))[:, None, :]
+    (meta_in,) = exchange([meta], gx, gy, 1)
+    answer = prolong[meta_in[:, 0, :per_peer].reshape(-1)].reshape(n, per_peer * cv, dof)
+    (fetched,) = exchange([answer], gx, gy, 2)
+    made = products(fetched.reshape(slots, cv, dof), stiffness, col_slot, group)
+    flat = made.reshape(slots // group, cv, group, bps * cv).transpose(0, 2, 1, 3)
+    (flat,) = exchange([flat.reshape(n, per_peer * cv, bps * cv)], gx, gy, 3)
+    flat = flat.reshape(slots // group, group, cv, bps * cv).transpose(0, 2, 1, 3)
+    part = flat.reshape(slots // group, cv, group * bps * cv)
+    code, factor = gathered_rows(part, meta_in, coarse_owner[:, 0], n, send_max, group, bps, per_peer)
     return delivered(code, factor, cv, gx, gy)
 
 

time: 138 us -> 126 us (0.913)
  Pallas kernels: 129 us -> 118 us
  local copies, waits for them, and re-layouts: 8.33 us -> 6.22 us
    pallas_call x2, Pallas kernels: 75.8 us -> 55.9 us  [the longest x1 43 us: handed(): pl.pallas_call(functools.partial(handed_kernel, (gx, gy, send_max)), out_...]
    pallas_call x1, Pallas kernels: 53.3 us -> 62.1 us  [fused(): pl.pallas_call(functools.partial(fused_kernel, (gx, gy, cv, bps, group)),...]
    unnamed x11 -> x6, local copies, waits for them, and re-layouts: 6.89 us -> 4.66 us
where the time goes in v1:
time: 126 us; the launch traced here: 124 us
  Pallas kernels  118 us (94%)
  local copies, waits for them, and re-layouts  6.22 us (5%)
    pallas_call x1, Pallas kernels, fused(): pl.pallas_call(functools.partial(fused_kernel, (gx, gy, cv, bps, group)),...  62.1 us
    pallas_call x1, Pallas kernels, handed(): pl.pallas_call(functools.partial(handed_kernel, (gx, gy, send_max)), out_...  43 us
    pallas_call x1, Pallas kernels, collected(): pl.pallas_call(functools.partial(collect_kernel, (gx, gy, cv, bps, group,...  12.9 us
    unnamed x6, local copies, waits for them, and re-layouts  4.66 us

profile of v1, /device:TPU:11, one launch (start us, length us, event | category | flops | bytes accessed | tf_op | source)
XLA Modules:
  0.0 124.4 jit_solution(4849445702041451649)
XLA Ops:
  0.0 0.7 pad.7.clone
  0.7 0.7 reshape.6
  1.5 0.8 copy.8
  2.3 0.1 reshape.7
  2.4 0.1 fusion
  2.4 0.1 add_add_fusion
  2.5 0.0 copy-start
  2.5 1.0 copy-done
  3.5 0.0 copy-start.1
  3.5 0.7 copy-done.1
  4.2 62.1 %fused.1 = (s32[32,1,128]{2,1,0:T(1,128)S(1)}, s16[32,2,24,384]{3,2,1,0:T(8,128)(2,1)S(1)}, f32[32,2,1,128]{3,2,1,0:T(1,128)S(1)}) custom-call(s32[4,128]{1,0:T(4,128)S(1)} %bitcast.4, s32[16,1,128]{2,1,0:T(1,128)S(1)} %bitcast.3, bf16[64,24,128]{2,1,0:T(8,128)(2,1)S(1)} %copy-done, bf16[128,4,128,128]{3,2,1,0:T(8,128)(2,1)} %stiff_ref.1), custom_call_target="tpu_custom_call" | custom-call | tf_op jit(solution)/shard_map/fused/pallas_call | solution.py:527
  66.3 12.9 %collected.1.total_ref = f32[129,24,384]{2,1,0:T(8,128)S(1)} custom-call(s32[32,1,128]{2,1,0:T(1,128)S(1)} %get-tuple-element.8.meta_ref, s16[32,2,24,384]{3,2,1,0:T(8,128)(2,1)S(1)} %get-tuple-element.9.part_ref, f32[32,2,1,128]{3,2,1,0:T(1,128)S(1)} %get-tuple-element.10.scale_ref), custom_call_target="tpu_custom_call" | custom-call | tf_op jit(solution)/shard_map/collected/pallas_call | solution.py:638
  79.2 43.0 %handed.1 = f32[128,24,384]{2,1,0:T(8,128)S(1)} custom-call(f32[129,24,384]{2,1,0:T(8,128)S(1)} %collected.1.total_ref), custom_call_target="tpu_custom_call" | custom-call | tf_op jit(solution)/shard_map/handed/pallas_call | solution.py:763
  122.3 2.2 %copy.10 = f32[128,24,384]{2,1,0:T(8,128)} copy(f32[128,24,384]{2,1,0:T(8,128)S(1)} %handed.1) | data formatting | bytes 9437184
  (1 shorter events, 0.0 us)
Async XLA Ops:
  2.5 1.0 copy-start
  3.5 0.7 copy-start.1

commit v2 on v0

--- a/solution.py
+++ b/solution.py
@@ -11,6 +11,7 @@
 AXES = ("gx", "gy")
 LANES = 128
 TOP = 32767.0
+ROWS = 8
 MESH = pl.DeviceIdType.MESH
 HBM = pl.BlockSpec(memory_space=pl.ANY)
 VMEM = pl.BlockSpec(memory_space=pltpu.VMEM)
@@ -198,9 +199,9 @@
     return jnp.sum(jnp.where(eye, column, 0.0), axis=0, keepdims=True)
 
 
-def as_column(row, rows):
+def as_column(row, rows, first=0):
     shape = (rows, LANES)
-    eye = lax.broadcasted_iota(jnp.int32, shape, 0) == lax.broadcasted_iota(jnp.int32, shape, 1)
+    eye = lax.broadcasted_iota(jnp.int32, shape, 0) + first == lax.broadcasted_iota(jnp.int32, shape, 1)
     return jnp.sum(jnp.where(eye, row, 0.0), axis=1, keepdims=True)
 
 
@@ -297,17 +298,128 @@
     )(col_slot, fetched, stiffness)
 
 
+def offset_at(i, side, sign, gx, gy):
+    half = gx // 2
+    x, y = lax.axis_index("gx"), lax.axis_index("gy")
+    row = lax.rem(lax.rem(x, half) + sign * (i // gy) + half, half)
+    col = lax.rem(y + sign * lax.rem(i, gy) + gy, gy)
+    return (side * half + row) * gy + col
+
+
+def mixed_at(k, sign, gx, gy):
+    count = gx // 2 * gy
+    near = lax.rem(k, 2)
+    side = lax.rem(lax.axis_index("gx") // (gx // 2) + 1 + near, 2)
+    return offset_at(lax.rem(k // 2 + near, count), side, sign, gx, gy)
+
+
+def arrival_at(k, gx, gy):
+    count = gx // 2 * gy
+    near = lax.rem(k, 2)
+    side = lax.rem(lax.axis_index("gx") // (gx // 2) + 1 + near, 2)
+    return offset_at(lax.rem(k // 2 + 1, count), side, -1, gx, gy)
+
+
+def slot_matrix(dims, meta_land, meta_flat, side, mine):
+    n, count, bps, group, send_max = dims
+    each = group + group * bps
+    square = (LANES, LANES)
+    sub = lax.broadcasted_iota(jnp.int32, square, 0)
+    lane = lax.broadcasted_iota(jnp.int32, square, 1)
+    for d in range(n):
+        meta_flat[d : d + 1] = meta_land[d]
+    flat = meta_flat[...].astype(jnp.float32).astype(jnp.bfloat16)
+    places = []
+    for kk in range(2):
+        owner = meta_land[kk * count + mine]
+        value = owner.astype(jnp.float32)
+        same = (as_column(value, LANES) == value) & (sub < lane) & (sub >= 2 * each)
+        rank = jnp.sum(jnp.where(same, 1.0, 0.0), axis=0, keepdims=True)
+        at = ((lax.rem(owner, count) * 2 + kk) * send_max).astype(jnp.float32) + rank
+        places.append(as_column(jnp.where(owner // count == side, at, -1.0), LANES))
+    second = lax.rem(lane // group, 2)
+    source = lax.broadcasted_iota(jnp.int32, (n, LANES), 0)
+    taken = lax.broadcasted_iota(jnp.int32, (n, LANES), 1) // (2 * group)
+    pick = jnp.where(sub == second * each + lax.rem(lane, group), 1.0, 0.0).astype(jnp.bfloat16)
+    every = jnp.dot(flat, pick, preferred_element_type=jnp.float32)
+    place = jnp.where(second == 0, places[0], places[1])
+    pieces = []
+    for half in range(2 * n * group // LANES):
+        first = half * (LANES // (2 * group))
+        asked = jnp.sum(jnp.where(source == taken + first, every, 0.0), axis=0, keepdims=True)
+        hit = sub.astype(jnp.float32) == asked + 2.0 * each
+        slot = jnp.sum(jnp.where(hit, place, 0.0), axis=0, keepdims=True)
+        pieces.append(jnp.where(sub.astype(jnp.float32) == slot, 1.0, 0.0))
+    return jnp.concatenate(pieces, axis=1).astype(jnp.bfloat16)
+
+
+def group_tail(dims, grp, slot_ref, wide_ref, cols_ref, proj_ref):
+    cv, bps, group = dims
+    span = bps * cv
+    lane = lax.broadcasted_iota(jnp.int32, (cv, LANES), 1)
+    for tl in range(group):
+        for q in range(bps):
+            block = wide_ref[slot_ref[q, grp * group + tl]]
+            at = (span * tl + cv * q) % LANES
+            first = min(cv, LANES - at)
+            cols_ref[tl, at : at + first, :] = block[:first]
+            if first < cv:
+                cols_ref[tl, 0 : cv - first, :] = block[first:]
+    ends = []
+    for tl in range(group):
+        cols = cols_ref[tl].astype(jnp.bfloat16)
+        prod = lax.dot_general(proj_ref[grp * group + tl], cols, NT, preferred_element_type=jnp.float32)
+        both = prod[:span] + prod[span:]
+        rel = (lane + (LANES * tl - span * tl) % LANES) % LANES
+        one = both[(bps - 1) * cv :]
+        for q in range(bps - 2, -1, -1):
+            one = jnp.where(rel < cv * (q + 1), both[q * cv : (q + 1) * cv], one)
+        ends.append(one)
+    tiles = []
+    for j in range(span * group // LANES):
+        low, high = LANES * j // span, (LANES * (j + 1) - 1) // span
+        tile = ends[high]
+        for tl in range(high - 1, low - 1, -1):
+            tile = jnp.where(lane < span * (tl + 1) - LANES * j, ends[tl], tile)
+        tiles.append(tile)
+    return jnp.concatenate(tiles, axis=1)
+
+
+def meta_row(dims, r, asked_row, pos_rows, owner_row):
+    count, bps, group = dims
+    each = group + group * bps
+    lane = lax.broadcasted_iota(jnp.int32, (1, LANES), 1)
+    row = owner_row[...]
+    for kk in range(2):
+        for tl in range(group):
+            t = (kk * count + r) * group + tl
+            row = jnp.where(lane == kk * each + tl, asked_row[0, t], row)
+            for q in range(bps):
+                row = jnp.where(lane == kk * each + group + tl * bps + q, pos_rows[q, t], row)
+    return row
+
+
 def fused_kernel(
     dims,
-    slot_ref, meta_ref, prolong_ref, stiff_ref,
-    meta_out, part_out, scale_out,
-    req_ref, stage_ref, fetched_ref, wide_ref, cols_ref, mats_ref, code_ref, factor_ref,
+    asked_ref, pos_ref, owner_ref, slot_in, prolong_in, stiff_ref,
+    out_ref,
+    asked_row, pos_rows, owner_row, slot_ref, prolong_ref, meta_ref,
+    meta_land, meta_flat, req_ref, stage_ref, fetched_ref, wide_ref, cols_ref, mats_ref, proj_ref,
+    code_ref, factor_ref, part_ref, scale_ref, select_ref, placed_ref, total_ref,
+    sent_ref, sent_scale, land_ref, land_scale, final_ref,
     meta_send, meta_recv, fetch_send, fetch_recv, part_send, part_recv, scale_send, scale_recv,
-    mats_sem, own_sem,
+    row_send, row_recv, unit_send, unit_recv, out_sem, mats_sem, own_sem,
 ):
-    gx, gy, cv, bps, group = dims
+    gx, gy, cv, bps, group, send_max = dims
     n = gx * gy
+    count = n // 2
+    span = bps * cv
+    width = group * span
+    each = group + group * bps
+    steps = cv // ROWS
+    slots = 2 * send_max
     me = lax.axis_index("gx") * gy + lax.axis_index("gy")
+    side, mine = me // count, lax.rem(me, count)
     barrier = pltpu.get_barrier_semaphore()
 
     def where(peer):
@@ -321,7 +433,8 @@
 
     def meta_copy(peer, source):
         return remote(
-            meta_ref.at[peer], meta_out.at[source], meta_send.at[peer], meta_recv.at[source], peer
+            meta_ref.at[lax.rem(peer, count)], meta_land.at[source],
+            meta_send.at[peer], meta_recv.at[source], peer,
         )
 
     def fetch_copy(peer, source):
@@ -331,13 +444,44 @@
             fetch_send.at[peer], fetch_recv.at[source], peer,
         )
 
-    def part_copies(peer, source):
+    def part_copy(h, peer, source):
+        return remote(
+            code_ref.at[lax.rem(peer, count), h], part_ref.at[source, h],
+            part_send.at[h, peer], part_recv.at[h, source], peer,
+        )
+
+    def scale_copy(peer, source):
+        return remote(
+            factor_ref.at[lax.rem(peer, count)], scale_ref.at[source],
+            scale_send.at[peer], scale_recv.at[source], peer,
+        )
+
+    def row_copies(h, peer, source):
+        device = side * count + peer
         return (
-            remote(code_ref.at[peer], part_out.at[source], part_send.at[peer], part_recv.at[source], peer),
             remote(
-                factor_ref.at[peer], scale_out.at[source], scale_send.at[peer], scale_recv.at[source], peer
+                sent_scale.at[h, peer], land_scale.at[h, source],
+                unit_send.at[h, peer], unit_recv.at[h, source], device,
+            ),
+            remote(
+                sent_ref.at[h, peer], land_ref.at[h, source],
+                row_send.at[h, peer], row_recv.at[h, source], device,
             ),
         )
+
+    def out_copies(source):
+        return [
+            pltpu.make_async_copy(
+                final_ref.at[source, pl.ds(kk * send_max, send_max)],
+                out_ref.at[pl.ds((kk * count + source) * send_max, send_max)],
+                out_sem.at[kk * count + source],
+            )
+            for kk in range(2)
+        ]
+
+    def by_turn(i, sign):
+        i = lax.rem(i, 2) * (count // 2) + i // 2
+        return lax.rem(offset_at(i, side, sign, gx, gy), count)
 
     def mats_copy(peer):
         return pltpu.make_async_copy(
@@ -350,141 +494,312 @@
         pl.semaphore_signal(barrier, inc=1, device_id=where(lax.rem(me + k, n)), device_id_type=MESH)
         return c
 
+    small = [
+        pltpu.make_async_copy(src, dst, own_sem.at[2 + i])
+        for i, (src, dst) in enumerate((
+            (asked_ref, asked_row), (pos_ref, pos_rows), (owner_ref, owner_row),
+            (prolong_in, prolong_ref), (slot_in, slot_ref),
+        ))
+    ]
+    for copy in small:
+        copy.start()
     lax.fori_loop(1, n, greet, 0)
-    own_meta = pltpu.make_async_copy(meta_ref.at[me], meta_out.at[me], own_sem.at[0])
+    for copy in small[:3]:
+        copy.wait()
+
+    def note(r, c):
+        meta_ref[r] = meta_row((count, bps, group), r, asked_row, pos_rows, owner_row)
+        return c
+
+    lax.fori_loop(0, count, note, 0, unroll=2)
+    own_meta = pltpu.make_async_copy(meta_ref.at[lax.rem(me, count)], meta_land.at[me], own_sem.at[0])
+    mats_copy(me).start()
+
+    def load(k, c):
+        mats_copy(mixed_at(k, -1, gx, gy)).start()
+        return c
+
+    lax.fori_loop(0, n - 1, load, 0)
     own_meta.start()
-
-    def load(k, c):
-        mats_copy(peer_at(k, gx, gy, False)).start()
-        return c
-
-    lax.fori_loop(0, n, load, 0)
     pl.semaphore_wait(barrier, n - 1)
 
     def ask(k, c):
-        meta_copy(peer_at(k, gx, gy, True), me).start()
+        meta_copy(mixed_at(k, 1, gx, gy), me).start()
         return c
 
     lax.fori_loop(0, n - 1, ask, 0)
     own_meta.wait()
 
     def asked(k, c):
-        source = peer_at(k, gx, gy, True)
+        source = mixed_at(k, -1, gx, gy)
         meta_copy(source, source).wait()
         return c
 
     lax.fori_loop(0, n - 1, asked, 0)
-    to_scalars = pltpu.make_async_copy(meta_out, req_ref, own_sem.at[1])
+    to_scalars = pltpu.make_async_copy(meta_land, req_ref, own_sem.at[1])
     to_scalars.start()
+    small[3].wait()
+    small[4].wait()
     to_scalars.wait()
+    first = side * each
 
     def fill(k, c):
-        peer = peer_at(k, gx, gy, True)
+        peer = mixed_at(k, 1, gx, gy)
         for j in range(group):
-            stage_ref[peer * group + j] = prolong_ref[req_ref[peer, 0, j]]
-        return c
-
-    lax.fori_loop(0, n, fill, 0)
+            stage_ref[peer * group + j] = prolong_ref[req_ref[peer, 0, first + j]]
+        return c
+
+    lax.fori_loop(0, n - 1, fill, 0)
+    for j in range(group):
+        stage_ref[me * group + j] = prolong_ref[req_ref[me, 0, first + j]]
 
     def answer(k, c):
-        fetch_copy(peer_at(k, gx, gy, True), me).start()
+        fetch_copy(mixed_at(k, 1, gx, gy), me).start()
         return c
 
     lax.fori_loop(0, n - 1, answer, 0)
-    for j in range(group):
-        wide_ref[me * group + j] = stage_ref[me * group + j].astype(jnp.float32)
+
+    def project(source, from_ref):
+        mats_copy(source).wait()
+        for j in range(group):
+            t = source * group + j
+            block = from_ref[t]
+            wide_ref[t] = block.astype(jnp.float32)
+            mats = mats_ref[t]
+            mats = jnp.concatenate([mats[q] for q in range(bps)], axis=1)
+            prod = jnp.dot(block, mats, preferred_element_type=jnp.float32)
+            rows = jnp.concatenate([prod[:, q * LANES : (q + 1) * LANES] for q in range(bps)], axis=0)
+            hi = rows.astype(jnp.bfloat16)
+            proj_ref[t, 0:span] = hi
+            proj_ref[t, span : 2 * span] = (rows - hi.astype(jnp.float32)).astype(jnp.bfloat16)
+
+    select_ref[...] = slot_matrix((n, count, bps, group, send_max), meta_land, meta_flat, side, mine)
+    project(me, stage_ref)
 
     def take(k, c):
-        source = peer_at(k, gx, gy, True)
-        fetch_copy(source, source).wait()
-        for j in range(group):
-            wide_ref[source * group + j] = fetched_ref[source * group + j].astype(jnp.float32)
+        source = mixed_at(k, -1, gx, gy)
+        fetch_copy(source, source).wait_recv()
+        project(source, fetched_ref)
         return c
 
     lax.fori_loop(0, n - 1, take, 0)
-    wide_step = 2 if n % 2 == 0 else 1
-
-    def work(i, c):
-        for u in range(wide_step):
-            mats_copy(peer_at(i * wide_step + u, gx, gy, False)).wait()
-        for u in range(wide_step):
-            peer = peer_at(i * wide_step + u, gx, gy, False)
-            out = group_product(
-                (cv, bps, group), peer, slot_ref, wide_ref, cols_ref.at[u],
-                lambda tl: mats_ref[peer * group + tl],
+
+    def send(h, j, both):
+        i = lax.rem(j + 1, count)
+        far = offset_at(i, 1 - side, 1, gx, gy)
+        near = offset_at(i, side, 1, gx, gy)
+        for peer in (far, near) if both else (far,):
+            if h == 0:
+                scale_copy(peer, me).start()
+            part_copy(h, peer, me).start()
+
+    def work(j, c):
+        at = lax.rem(offset_at(lax.rem(j + 1, count), side, 1, gx, gy), count)
+        for u in range(2):
+            out = group_tail(
+                (cv, bps, group), u * count + at, slot_ref, wide_ref, cols_ref.at[u], proj_ref
             )
-            code_ref[peer], factor_ref[peer] = coded(out)
-
-        @pl.when(i > 0)
+            top = jnp.maximum(jnp.max(jnp.abs(out), axis=1, keepdims=True), 1e-30)
+            code = jnp.round(out * (TOP / top)).astype(jnp.int32)
+            for h in range(steps):
+                code_ref[at, h, u] = code[h * ROWS : (h + 1) * ROWS].astype(jnp.int16)
+            factor_ref[at, u] = as_row(top * (1.0 / TOP))
+
+        @pl.when(j > 0)
         def _():
-            for u in range(wide_step):
-                for copy in part_copies(peer_at((i - 1) * wide_step + u, gx, gy, False), me):
-                    copy.start()
-
-        return c
-
-    lax.fori_loop(0, n // wide_step, work, 0)
-    for k in range(n - wide_step, n - 1):
-        for copy in part_copies(peer_at(k, gx, gy, False), me):
-            copy.start()
-    own = (
-        pltpu.make_async_copy(code_ref.at[me], part_out.at[me], own_sem.at[2]),
-        pltpu.make_async_copy(factor_ref.at[me], scale_out.at[me], own_sem.at[3]),
-    )
-    for copy in own:
-        copy.start()
+            send(0, j - 1, True)
+
+        return c
+
+    lax.fori_loop(0, count, work, 0)
+    send(0, count - 1, False)
+    for h in range(1, steps):
+
+        def more(j, c):
+            send(h, j, True)
+            return c
+
+        lax.fori_loop(0, count - 1, more, 0)
+        send(h, count - 1, False)
+
+    lane = lax.broadcasted_iota(jnp.int32, (ROWS, LANES), 1)
+    column = [(lane + LANES * j) // cv for j in range(width // LANES)]
+
+    def place(h, d, from_ref, from_scale, at):
+        blocks = []
+        for kk in range(2):
+            v = from_ref[at, h, kk].astype(jnp.int32).astype(jnp.float32)
+            v = v * as_column(from_scale[at, kk], ROWS, h * ROWS)
+            for tl in range(group):
+                begin = span * tl
+                low, high = begin // LANES * LANES, (begin + span - 1) // LANES * LANES
+                x = v[:, low : low + LANES]
+                if high > low:
+                    x = jnp.where(lane >= begin % LANES, x, v[:, high : high + LANES])
+                tiles = [jnp.zeros((ROWS, LANES), jnp.float32) for _ in column]
+                for q in range(bps):
+                    pos = req_ref[d, 0, kk * each + group + tl * bps + q]
+                    moved = pltpu.roll(x, lax.rem(cv * pos + 8 * LANES - begin - cv * q, LANES), 1)
+                    tiles = [jnp.where(col == pos, moved, tile) for col, tile in zip(column, tiles)]
+                blocks.append(jnp.concatenate(tiles, axis=1))
+        rows = pl.ds(pl.multiple_of(d * ROWS, ROWS), ROWS)
+        placed_ref[:, rows, :] = jnp.swapaxes(jnp.stack(blocks), 0, 1)
+
+    def decode(h, source, from_ref, from_scale):
+        values = from_ref[h, source].astype(jnp.int32).astype(jnp.float32)
+        values = values * as_column(from_scale[h, source], slots * ROWS)
+        final_ref[source, :, h * ROWS : (h + 1) * ROWS, :] = values.reshape(slots, ROWS, width)
+        if h == steps - 1:
+            for copy in out_copies(source):
+                copy.start()
+
+    def decode_all(h):
+        decode(h, mine, sent_ref, sent_scale)
+
+        def one(i, c):
+            source = by_turn(i, -1)
+            for copy in row_copies(h, source, source):
+                copy.wait_recv()
+            decode(h, source, land_ref, land_scale)
+            return c
+
+        lax.fori_loop(1, count, one, 0)
+
+    for h in range(steps):
+        place(h, me, code_ref, factor_ref, mine)
+
+        def arrive(k, c):
+            source = arrival_at(k, gx, gy)
+            if h == 0:
+                scale_copy(source, source).wait_recv()
+            part_copy(h, source, source).wait_recv()
+            place(h, source, part_ref, scale_ref, source)
+            return c
+
+        lax.fori_loop(0, n - 1, arrive, 0)
+
+        def gather(r, c):
+            x = placed_ref[r]
+            hi = x.astype(jnp.bfloat16)
+            lo = (x - hi.astype(jnp.float32)).astype(jnp.bfloat16)
+            select = select_ref[...]
+            got = jnp.dot(select, hi, preferred_element_type=jnp.float32)
+            got = got + jnp.dot(select, lo, preferred_element_type=jnp.float32)
+            total_ref[r] = got
+            return c
+
+        lax.fori_loop(0, ROWS, gather, 0)
+
+        def pack(i):
+            peer = by_turn(i, 1)
+            values = total_ref[:, pl.ds(pl.multiple_of(peer * slots, slots), slots), :]
+            values = jnp.swapaxes(values, 0, 1).reshape(slots * ROWS, width)
+            sent_ref[h, peer], sent_scale[h, peer] = coded(values)
+
+        def hand(i):
+            for copy in row_copies(h, by_turn(i, 1), mine):
+                copy.start()
+
+        pack(1)
+
+        def pass_on(i, c):
+            pack(i)
+            hand(i - 1)
+            return c
+
+        lax.fori_loop(2, count, pass_on, 0)
+        pack(0)
+        hand(count - 1)
+        if h > 0:
+            decode_all(h - 1)
+    decode_all(steps - 1)
 
     def drain(k, c):
-        source = peer_at(k, gx, gy, False)
-        for copy in part_copies(source, source):
+        peer = mixed_at(k, 1, gx, gy)
+        fetch_copy(peer, me).wait_send()
+        scale_copy(peer, me).wait_send()
+        for h in range(steps):
+            part_copy(h, peer, me).wait_send()
+        return c
+
+    lax.fori_loop(0, n - 1, drain, 0)
+
+    def finish(i, c):
+        for h in range(steps):
+            for copy in row_copies(h, by_turn(i, 1), mine):
+                copy.wait_send()
+        return c
+
+    lax.fori_loop(1, count, finish, 0)
+
+    def written(i, c):
+        for copy in out_copies(i):
             copy.wait()
         return c
 
-    lax.fori_loop(0, n - 1, drain, 0)
-    for copy in own:
-        copy.wait()
-
-
-def fused(meta, prolong, stiffness, col_slot, gx, gy, group):
+    lax.fori_loop(0, count, written, 0)
+
+
+def fused(asked, pos, owners, slots_of, prolong, stiffness, gx, gy, group, send_max):
     slots, bps, dof, _ = stiffness.shape
     cv = prolong.shape[1]
     n = gx * gy
+    count = n // 2
     width = group * bps * cv
+    steps = cv // ROWS
+    taken = 2 * n * group
+    rows = 2 * send_max * ROWS
     sem = pltpu.SemaphoreType.DMA
     return pl.pallas_call(
-        functools.partial(fused_kernel, (gx, gy, cv, bps, group)),
-        out_shape=[
-            jax.ShapeDtypeStruct(meta.shape, jnp.int32),
-            jax.ShapeDtypeStruct((n, cv, width), jnp.int16),
-            jax.ShapeDtypeStruct((n, 1, LANES), jnp.float32),
-        ],
-        in_specs=[SMEM, VMEM, VMEM, HBM],
-        out_specs=[VMEM, VMEM, VMEM],
+        functools.partial(fused_kernel, (gx, gy, cv, bps, group, send_max)),
+        out_shape=jax.ShapeDtypeStruct((n * send_max, cv, width), jnp.float32),
+        in_specs=[HBM] * 6,
+        out_specs=HBM,
         scratch_shapes=[
-            pltpu.SMEM(meta.shape, jnp.int32),
+            pltpu.SMEM(asked.shape, jnp.int32),
+            pltpu.SMEM(pos.shape, jnp.int32),
+            pltpu.VMEM(owners.shape, jnp.int32),
+            pltpu.SMEM(slots_of.shape, jnp.int32),
+            pltpu.VMEM(prolong.shape, jnp.bfloat16),
+            pltpu.VMEM((count, 1, LANES), jnp.int32),
+            pltpu.VMEM((n, 1, LANES), jnp.int32),
+            pltpu.VMEM((n, LANES), jnp.int32),
+            pltpu.SMEM((n, 1, LANES), jnp.int32),
             pltpu.VMEM((slots, cv, dof), jnp.bfloat16),
             pltpu.VMEM((slots, cv, dof), jnp.bfloat16),
             pltpu.VMEM((slots, cv, dof), jnp.float32),
             pltpu.VMEM((2, group, LANES, dof), jnp.float32),
             pltpu.VMEM((slots, bps, dof, dof), jnp.bfloat16),
-            pltpu.VMEM((n, cv, width), jnp.int16),
-            pltpu.VMEM((n, 1, LANES), jnp.float32),
+            pltpu.VMEM((slots, 2 * bps * cv, dof), jnp.bfloat16),
+            pltpu.VMEM((count, steps, 2, ROWS, width), jnp.int16),
+            pltpu.VMEM((count, 2, 1, LANES), jnp.float32),
+            pltpu.VMEM((n, steps, 2, ROWS, width), jnp.int16),
+            pltpu.VMEM((n, 2, 1, LANES), jnp.float32),
+            pltpu.VMEM((n * send_max, taken), jnp.bfloat16),
+            pltpu.VMEM((ROWS, taken, width), jnp.float32),
+            pltpu.VMEM((ROWS, n * send_max, width), jnp.float32),
+            pltpu.VMEM((steps, count, rows, width), jnp.int16),
+            pltpu.VMEM((steps, count, 1, LANES), jnp.float32),
+            pltpu.VMEM((steps, count, rows, width), jnp.int16),
+            pltpu.VMEM((steps, count, 1, LANES), jnp.float32),
+            pltpu.VMEM((count, 2 * send_max, cv, width), jnp.float32),
         ]
-        + [sem((n,))] * 9
-        + [sem((4,))],
+        + [sem((n,))] * 4
+        + [sem((steps, n))] * 2
+        + [sem((n,))] * 2
+        + [sem((steps, count))] * 4
+        + [sem((n,))] * 2
+        + [sem((7,))],
         compiler_params=pltpu.CompilerParams(
-            collective_id=1, has_side_effects=True, vmem_limit_bytes=56 << 20
+            collective_id=1, has_side_effects=True, vmem_limit_bytes=54 << 20
         ),
         name="fused",
-    )(col_slot, meta, prolong, stiffness)
+    )(asked, pos, owners, slots_of, prolong, stiffness)
 
 
 def gather_rows_kernel(dims, meta_ref, owner_ref, part_ref, *refs):
-    cv, bps, per_peer, group, send_max, quant = dims
-    if quant:
-        scale_ref, out_ref, out_scale_ref, total_ref, place_ref, seen_ref = refs
-    else:
-        out_ref, out_scale_ref, total_ref, place_ref, seen_ref = refs
+    cv, bps, per_peer, group, send_max = dims
+    out_ref, out_scale_ref, total_ref, place_ref, seen_ref = refs
     n = out_ref.shape[0]
     groups, _, width = part_ref.shape
     span = width // group
@@ -515,20 +830,14 @@
             pos = meta_ref[t // per_peer, 0, per_peer + (t % per_peer) * bps + j % bps]
             at = at + jnp.where(row_lane // cv == j, cv * (pos - j), 0)
         hot = jnp.where(column == at, 1.0, 0.0).astype(jnp.bfloat16)
-        if quant:
-            code = part_ref[g].astype(jnp.int32)
-            high = code >> 8
-            pieces = [high.astype(jnp.float32), (code - high * 256).astype(jnp.float32)]
-            weights = [256.0, 1.0]
-        else:
-            rest = part_ref[g]
-            pieces, weights = [], [1.0, 1.0, 1.0]
-            for _ in range(3):
-                piece = rest.astype(jnp.bfloat16).astype(jnp.float32)
-                pieces.append(piece)
-                rest = rest - piece
+        rest = part_ref[g]
+        pieces = []
+        for _ in range(3):
+            piece = rest.astype(jnp.bfloat16).astype(jnp.float32)
+            pieces.append(piece)
+            rest = rest - piece
         placed = 0.0
-        for piece, weight in zip(pieces, weights):
+        for piece in pieces:
             stack = jnp.concatenate(
                 [
                     jnp.where((lane >= span * tl) & (lane < span * (tl + 1)), piece, 0.0)
@@ -536,17 +845,13 @@
                 ],
                 axis=0,
             ).astype(jnp.bfloat16)
-            placed = placed + weight * lax.dot_general(
+            placed = placed + lax.dot_general(
                 stack, hot, NT, preferred_element_type=jnp.float32
             )
-        if quant:
-            factor = as_column(scale_ref[g], cv)
         for tl in range(group):
             t = g * group + tl
             where = place_ref[meta_ref[t // per_peer, 0, t % per_peer]]
             rows = placed[tl * cv : (tl + 1) * cv]
-            if quant:
-                rows = rows * factor
             total_ref[where] = total_ref[where] + rows
         return c
 
@@ -560,17 +865,15 @@
     lax.fori_loop(0, n, emit, 0, unroll=4)
 
 
-def gathered_rows(part, scale, meta, owners, n, send_max, group, bps, per_peer):
+def gathered_rows(part, meta, owners, n, send_max, group, bps, per_peer):
     groups, cv, width = part.shape
-    quant = scale is not None
-    args = [meta, owners, part] + ([scale] if quant else [])
     return pl.pallas_call(
-        functools.partial(gather_rows_kernel, (cv, bps, per_peer, group, send_max, quant)),
+        functools.partial(gather_rows_kernel, (cv, bps, per_peer, group, send_max)),
         out_shape=[
             jax.ShapeDtypeStruct((n, send_max * cv, width), jnp.int16),
             jax.ShapeDtypeStruct((n, 1, LANES), jnp.float32),
         ],
-        in_specs=[SMEM, SMEM] + [VMEM] * (len(args) - 2),
+        in_specs=[SMEM, SMEM, VMEM],
         out_specs=[VMEM, VMEM],
         scratch_shapes=[
             pltpu.VMEM((n * send_max, cv, width), jnp.float32),
@@ -579,7 +882,7 @@
         ],
         compiler_params=pltpu.CompilerParams(vmem_limit_bytes=48 << 20),
         name="gathered_rows",
-    )(*args)
+    )(meta, owners, part)
 
 
 def per_device(gx, gy, prolong, stiffness, request, col_slot, col_pos, coarse_owner):
@@ -588,25 +891,26 @@
     slots, bps = col_slot.shape
     per_peer = slots // n
     group = MAXNB // bps
-    quant = per_peer == group
     send_max = (2 * own_aggs + n - 1) // n
-
+    each = per_peer + per_peer * bps
+    halved = per_peer == group and gx % 2 == 0 and slots == LANES and cv % ROWS == 0 and 2 * group == ROWS == 2 * send_max and 2 * each + own_aggs <= LANES
+
+    if halved:
+        owners = jnp.pad(coarse_owner.T, ((0, 0), (2 * each, LANES - own_aggs - 2 * each)))
+        held = (request[None], col_pos.T, owners, col_slot.T, prolong, stiffness)
+        held = [pltpu.with_memory_space_constraint(a, pltpu.HBM) for a in held]
+        return fused(*held, gx, gy, group, send_max)
     meta = jnp.concatenate([request.reshape(n, per_peer), col_pos.reshape(n, per_peer * bps)], axis=1)
-    meta = jnp.pad(meta, ((0, 0), (0, LANES - meta.shape[1])))[:, None, :]
-    if quant:
-        meta_in, part, scale = fused(meta, prolong, stiffness, col_slot, gx, gy, group)
-    else:
-        (meta_in,) = exchange([meta], gx, gy, 1)
-        answer = prolong[meta_in[:, 0, :per_peer].reshape(-1)].reshape(n, per_peer * cv, dof)
-        (fetched,) = exchange([answer], gx, gy, 2)
-        made = products(fetched.reshape(slots, cv, dof), stiffness, col_slot, group)
-        flat = made.reshape(slots // group, cv, group, bps * cv).transpose(0, 2, 1, 3)
-        (flat,) = exchange([flat.reshape(n, per_peer * cv, bps * cv)], gx, gy, 3)
-        flat = flat.reshape(slots // group, group, cv, bps * cv).transpose(0, 2, 1, 3)
-        part, scale = flat.reshape(slots // group, cv, group * bps * cv), None
-    code, factor = gathered_rows(
-        part, scale, meta_in, coarse_owner[:, 0], n, send_max, group, bps, per_peer
-    )
+    meta = jnp.pad(meta, ((0, 0), (0, LANES - each)))[:, None, :]
+    (meta_in,) = exchange([meta], gx, gy, 1)
+    answer = prolong[meta_in[:, 0, :per_peer].reshape(-1)].reshape(n, per_peer * cv, dof)
+    (fetched,) = exchange([answer], gx, gy, 2)
+    made = products(fetched.reshape(slots, cv, dof), stiffness, col_slot, group)
+    flat = made.reshape(slots // group, cv, group, bps * cv).transpose(0, 2, 1, 3)
+    (flat,) = exchange([flat.reshape(n, per_peer * cv, bps * cv)], gx, gy, 3)
+    flat = flat.reshape(slots // group, group, cv, bps * cv).transpose(0, 2, 1, 3)
+    part = flat.reshape(slots // group, cv, group * bps * cv)
+    code, factor = gathered_rows(part, meta_in, coarse_owner[:, 0], n, send_max, group, bps, per_peer)
     return delivered(code, factor, cv, gx, gy)
 
 

time: 138 us -> 101 us (0.73); the launches traced: 138 us -> 98.8 us
  Pallas kernels: 129 us -> 92.7 us
  local copies, waits for them, and re-layouts: 8.33 us -> 6.06 us
    pallas_call x3 -> x1, Pallas kernels: 129 us -> 92.7 us  [fused(): pl.pallas_call(functools.partial(fused_kernel, (gx, gy, cv, bps, group, s...]
    unnamed x11 -> x1, local copies, waits for them, and re-layouts: 6.89 us -> 4.83 us
where the time goes in v2:
time: 101 us; the launch traced here: 98.8 us
  Pallas kernels  92.7 us (92%)
  local copies, waits for them, and re-layouts  6.06 us (6%)
    pallas_call x1, Pallas kernels, fused(): pl.pallas_call(functools.partial(fused_kernel, (gx, gy, cv, bps, group, s...  92.7 us
    unnamed x1, local copies, waits for them, and re-layouts  4.83 us

profile of v2, /device:TPU:11, one launch (start us, length us, event | category | flops | bytes accessed | tf_op | source)
XLA Modules:
  0.0 98.8 jit_solution(13982911716207575610)
XLA Ops:
  0.0 1.2 %pad.4.owner_ref = s32[1,128]{1,0:T(1,128)} pad(s32[1,64]{1,0:T(1,128)} %bitcast.7, s32[]{:T(128)} %constant.0.clone.1), padding=0_0x40_24 | pad | bytes 772 | tf_op jit(solution)/shard_map/jit(_pad)/pad | solution.py:899
  1.2 92.7 %fused.1 = f32[128,24,384]{2,1,0:T(8,128)} custom-call(s32[1,128]{1,0:T(1,128)} %bitcast.6, s32[4,128]{1,0:T(4,128)} %bitcast.4, s32[1,128]{1,0:T(1,128)} %pad.4.owner_ref, s32[4,128]{1,0:T(4,128)} %bitcast.5, bf16[64,24,128]{2,1,0:T(8,128)(2,1)} %prolong_in.1, bf16[128,4,128,128]{3,2,1,0:T(8,128)(2,1)} %stiff_ref.1), custom_call_target="tpu_custom_call" | custom-call | tf_op jit(solution)/shard_map/fused/pallas_call | solution.py:753
  93.9 4.8 %copy.8 = f32[128,24,384]{2,1,0:T(8,128)} copy(f32[128,24,384]{2,1,0:T(8,128)} %fused.1) | data formatting | bytes 9437184

commit v3 on v2

--- a/solution.py
+++ b/solution.py
@@ -12,6 +12,8 @@
 LANES = 128
 TOP = 32767.0
 ROWS = 8
+PAIR = 1
+DEEP = 1
 MESH = pl.DeviceIdType.MESH
 HBM = pl.BlockSpec(memory_space=pl.ANY)
 VMEM = pl.BlockSpec(memory_space=pltpu.VMEM)
@@ -313,13 +315,6 @@
     return offset_at(lax.rem(k // 2 + near, count), side, sign, gx, gy)
 
 
-def arrival_at(k, gx, gy):
-    count = gx // 2 * gy
-    near = lax.rem(k, 2)
-    side = lax.rem(lax.axis_index("gx") // (gx // 2) + 1 + near, 2)
-    return offset_at(lax.rem(k // 2 + 1, count), side, -1, gx, gy)
-
-
 def slot_matrix(dims, meta_land, meta_flat, side, mine):
     n, count, bps, group, send_max = dims
     each = group + group * bps
@@ -385,17 +380,16 @@
     return jnp.concatenate(tiles, axis=1)
 
 
-def meta_row(dims, r, asked_row, pos_rows, owner_row):
-    count, bps, group = dims
+def meta_row(dims, r, asked_row, pos_rows, row):
+    count, bps, group, cv = dims
     each = group + group * bps
     lane = lax.broadcasted_iota(jnp.int32, (1, LANES), 1)
-    row = owner_row[...]
     for kk in range(2):
         for tl in range(group):
             t = (kk * count + r) * group + tl
             row = jnp.where(lane == kk * each + tl, asked_row[0, t], row)
             for q in range(bps):
-                row = jnp.where(lane == kk * each + group + tl * bps + q, pos_rows[q, t], row)
+                row = jnp.where(lane == kk * each + group + tl * bps + q, pos_rows[q, t] * cv, row)
     return row
 
 
@@ -469,12 +463,13 @@
             ),
         )
 
-    def out_copies(source):
+    def out_copies(h, source):
+        rows = pl.ds(h * ROWS, ROWS)
         return [
             pltpu.make_async_copy(
-                final_ref.at[source, pl.ds(kk * send_max, send_max)],
-                out_ref.at[pl.ds((kk * count + source) * send_max, send_max)],
-                out_sem.at[kk * count + source],
+                final_ref.at[source, pl.ds(kk * send_max, send_max), rows],
+                out_ref.at[pl.ds((kk * count + source) * send_max, send_max), rows],
+                out_sem.at[h, kk * count + source],
             )
             for kk in range(2)
         ]
@@ -506,9 +501,13 @@
     lax.fori_loop(1, n, greet, 0)
     for copy in small[:3]:
         copy.wait()
+    owners = jnp.zeros((1, LANES), jnp.int32)
+    for a in range(owner_row.shape[1]):
+        at = lax.broadcasted_iota(jnp.int32, (1, LANES), 1) == 2 * each + a
+        owners = jnp.where(at, owner_row[0, a], owners)
 
     def note(r, c):
-        meta_ref[r] = meta_row((count, bps, group), r, asked_row, pos_rows, owner_row)
+        meta_ref[r] = meta_row((count, bps, group, cv), r, asked_row, pos_rows, owners)
         return c
 
     lax.fori_loop(0, count, note, 0, unroll=2)
@@ -593,26 +592,31 @@
                 scale_copy(peer, me).start()
             part_copy(h, peer, me).start()
 
-    def work(j, c):
-        at = lax.rem(offset_at(lax.rem(j + 1, count), side, 1, gx, gy), count)
-        for u in range(2):
-            out = group_tail(
-                (cv, bps, group), u * count + at, slot_ref, wide_ref, cols_ref.at[u], proj_ref
-            )
-            top = jnp.maximum(jnp.max(jnp.abs(out), axis=1, keepdims=True), 1e-30)
-            code = jnp.round(out * (TOP / top)).astype(jnp.int32)
-            for h in range(steps):
-                code_ref[at, h, u] = code[h * ROWS : (h + 1) * ROWS].astype(jnp.int16)
-            factor_ref[at, u] = as_row(top * (1.0 / TOP))
-
-        @pl.when(j > 0)
+    def work(g, c):
+        for v in range(DEEP):
+            at = lax.rem(offset_at(lax.rem(g * DEEP + v + 1, count), side, 1, gx, gy), count)
+            for u in range(2):
+                out = group_tail(
+                    (cv, bps, group), u * count + at, slot_ref, wide_ref, cols_ref.at[2 * v + u], proj_ref
+                )
+                top = jnp.maximum(jnp.max(jnp.abs(out), axis=1, keepdims=True), 1e-30)
+                code = jnp.round(out * (TOP / top)).astype(jnp.int32)
+                for h in range(steps):
+                    code_ref[at, h, u] = code[h * ROWS : (h + 1) * ROWS].astype(jnp.int16)
+                factor_ref[at, u] = as_row(top * (1.0 / TOP))
+
+        @pl.when(g > 0)
         def _():
-            send(0, j - 1, True)
-
-        return c
-
-    lax.fori_loop(0, count, work, 0)
-    send(0, count - 1, False)
+            for v in range(DEEP):
+                send(0, (g - 1) * DEEP + v, True)
+
+        return c
+
+    lax.fori_loop(0, count // DEEP, work, 0)
+    for v in range(DEEP):
+        send(0, count - DEEP + v, v < DEEP - 1)
+    part_ref[me] = code_ref[mine]
+    scale_ref[me] = factor_ref[mine]
     for h in range(1, steps):
 
         def more(j, c):
@@ -623,13 +627,12 @@
         send(h, count - 1, False)
 
     lane = lax.broadcasted_iota(jnp.int32, (ROWS, LANES), 1)
-    column = [(lane + LANES * j) // cv for j in range(width // LANES)]
-
-    def place(h, d, from_ref, from_scale, at):
-        blocks = []
+    column = [(lane + LANES * j) // cv * cv for j in range(width // LANES)]
+
+    def place(h, d):
         for kk in range(2):
-            v = from_ref[at, h, kk].astype(jnp.int32).astype(jnp.float32)
-            v = v * as_column(from_scale[at, kk], ROWS, h * ROWS)
+            v = part_ref[d, h, kk].astype(jnp.int32).astype(jnp.float32)
+            v = v * as_column(scale_ref[d, kk], ROWS, h * ROWS)
             for tl in range(group):
                 begin = span * tl
                 low, high = begin // LANES * LANES, (begin + span - 1) // LANES * LANES
@@ -639,77 +642,106 @@
                 tiles = [jnp.zeros((ROWS, LANES), jnp.float32) for _ in column]
                 for q in range(bps):
                     pos = req_ref[d, 0, kk * each + group + tl * bps + q]
-                    moved = pltpu.roll(x, lax.rem(cv * pos + 8 * LANES - begin - cv * q, LANES), 1)
+                    moved = pltpu.roll(x, (pos + (-begin - cv * q) % LANES) & (LANES - 1), 1)
                     tiles = [jnp.where(col == pos, moved, tile) for col, tile in zip(column, tiles)]
-                blocks.append(jnp.concatenate(tiles, axis=1))
-        rows = pl.ds(pl.multiple_of(d * ROWS, ROWS), ROWS)
-        placed_ref[:, rows, :] = jnp.swapaxes(jnp.stack(blocks), 0, 1)
-
-    def decode(h, source, from_ref, from_scale):
-        values = from_ref[h, source].astype(jnp.int32).astype(jnp.float32)
-        values = values * as_column(from_scale[h, source], slots * ROWS)
+                p = (d * 2 + kk) * group + tl
+                for j, tile in enumerate(tiles):
+                    placed_ref[j, pl.ds(pl.multiple_of(p * ROWS, ROWS), ROWS), :] = tile
+
+    def decode(h, source):
+        values = land_ref[h, source].astype(jnp.int32).astype(jnp.float32)
+        values = values * as_column(land_scale[h, source], slots * ROWS)
         final_ref[source, :, h * ROWS : (h + 1) * ROWS, :] = values.reshape(slots, ROWS, width)
-        if h == steps - 1:
-            for copy in out_copies(source):
-                copy.start()
 
     def decode_all(h):
-        decode(h, mine, sent_ref, sent_scale)
-
-        def one(i, c):
-            source = by_turn(i, -1)
-            for copy in row_copies(h, source, source):
-                copy.wait_recv()
-            decode(h, source, land_ref, land_scale)
+        def some(g, c):
+            turns = [lax.rem(g * PAIR + u, count) for u in range(1, PAIR + 1)]
+            sources = [by_turn(i, -1) for i in turns]
+            for i, source in zip(turns, sources):
+
+                @pl.when(i > 0)
+                def _():
+                    for copy in row_copies(h, source, source):
+                        copy.wait_recv()
+
+            for source in sources:
+                decode(h, source)
+            for source in sources:
+                for copy in out_copies(h, source):
+                    copy.start()
             return c
 
-        lax.fori_loop(1, count, one, 0)
+        lax.fori_loop(0, count // PAIR, some, 0)
 
     for h in range(steps):
-        place(h, me, code_ref, factor_ref, mine)
-
-        def arrive(k, c):
-            source = arrival_at(k, gx, gy)
-            if h == 0:
-                scale_copy(source, source).wait_recv()
-            part_copy(h, source, source).wait_recv()
-            place(h, source, part_ref, scale_ref, source)
+
+        def arrive(g, c):
+            turns = [lax.rem(g * PAIR + u, count) for u in range(1, PAIR + 1)]
+            sources = []
+            for i in turns:
+                at = lax.rem(offset_at(i, side, -1, gx, gy), count)
+                far, near = (1 - side) * count + at, side * count + at
+
+                def landed(source):
+                    if h == 0:
+                        scale_copy(source, source).wait_recv()
+                    part_copy(h, source, source).wait_recv()
+
+                landed(far)
+
+                @pl.when(i > 0)
+                def _():
+                    landed(near)
+
+                sources += [far, near]
+            for source in sources:
+                place(h, source)
             return c
 
-        lax.fori_loop(0, n - 1, arrive, 0)
-
-        def gather(r, c):
-            x = placed_ref[r]
-            hi = x.astype(jnp.bfloat16)
-            lo = (x - hi.astype(jnp.float32)).astype(jnp.bfloat16)
+        lax.fori_loop(0, count // PAIR, arrive, 0)
+
+        def gather(g, c):
             select = select_ref[...]
-            got = jnp.dot(select, hi, preferred_element_type=jnp.float32)
-            got = got + jnp.dot(select, lo, preferred_element_type=jnp.float32)
-            total_ref[r] = got
+            for u in range(PAIR):
+                rows = pl.ds(g * PAIR + u, 2 * n * group, stride=ROWS)
+                x = jnp.concatenate([placed_ref[j, rows, :] for j in range(len(column))], axis=1)
+                hi = x.astype(jnp.bfloat16)
+                lo = (x - hi.astype(jnp.float32)).astype(jnp.bfloat16)
+                got = jnp.dot(select, hi, preferred_element_type=jnp.float32)
+                total_ref[g * PAIR + u] = got + jnp.dot(select, lo, preferred_element_type=jnp.float32)
             return c
 
-        lax.fori_loop(0, ROWS, gather, 0)
-
-        def pack(i):
+        lax.fori_loop(0, ROWS // PAIR, gather, 0)
+
+        def pack(i, own):
             peer = by_turn(i, 1)
             values = total_ref[:, pl.ds(pl.multiple_of(peer * slots, slots), slots), :]
             values = jnp.swapaxes(values, 0, 1).reshape(slots * ROWS, width)
-            sent_ref[h, peer], sent_scale[h, peer] = coded(values)
+            code, scale = coded(values)
+            if own:
+                land_ref[h, mine], land_scale[h, mine] = code, scale
+            else:
+                sent_ref[h, peer], sent_scale[h, peer] = code, scale
 
         def hand(i):
             for copy in row_copies(h, by_turn(i, 1), mine):
                 copy.start()
 
-        pack(1)
-
-        def pass_on(i, c):
-            pack(i)
-            hand(i - 1)
+        for u in range(1, PAIR + 1):
+            pack(u, False)
+
+        def pass_on(g, c):
+            for u in range(1, PAIR + 1):
+                pack(g * PAIR + u, False)
+            for u in range(1, PAIR + 1):
+                hand(g * PAIR - PAIR + u)
             return c
 
-        lax.fori_loop(2, count, pass_on, 0)
-        pack(0)
-        hand(count - 1)
+        lax.fori_loop(1, count // PAIR - 1, pass_on, 0)
+        for u in range(count - PAIR + 1, count + 1):
+            pack(u % count, u == count)
+        for u in range(count - 2 * PAIR + 1, count):
+            hand(u)
         if h > 0:
             decode_all(h - 1)
     decode_all(steps - 1)
@@ -733,8 +765,9 @@
     lax.fori_loop(1, count, finish, 0)
 
     def written(i, c):
-        for copy in out_copies(i):
-            copy.wait()
+        for h in range(steps):
+            for copy in out_copies(h, i):
+                copy.wait()
         return c
 
     lax.fori_loop(0, count, written, 0)
@@ -758,7 +791,7 @@
         scratch_shapes=[
             pltpu.SMEM(asked.shape, jnp.int32),
             pltpu.SMEM(pos.shape, jnp.int32),
-            pltpu.VMEM(owners.shape, jnp.int32),
+            pltpu.SMEM(owners.shape, jnp.int32),
             pltpu.SMEM(slots_of.shape, jnp.int32),
             pltpu.VMEM(prolong.shape, jnp.bfloat16),
             pltpu.VMEM((count, 1, LANES), jnp.int32),
@@ -768,7 +801,7 @@
             pltpu.VMEM((slots, cv, dof), jnp.bfloat16),
             pltpu.VMEM((slots, cv, dof), jnp.bfloat16),
             pltpu.VMEM((slots, cv, dof), jnp.float32),
-            pltpu.VMEM((2, group, LANES, dof), jnp.float32),
+            pltpu.VMEM((2 * DEEP, group, LANES, dof), jnp.float32),
             pltpu.VMEM((slots, bps, dof, dof), jnp.bfloat16),
             pltpu.VMEM((slots, 2 * bps * cv, dof), jnp.bfloat16),
             pltpu.VMEM((count, steps, 2, ROWS, width), jnp.int16),
@@ -776,7 +809,7 @@
             pltpu.VMEM((n, steps, 2, ROWS, width), jnp.int16),
             pltpu.VMEM((n, 2, 1, LANES), jnp.float32),
             pltpu.VMEM((n * send_max, taken), jnp.bfloat16),
-            pltpu.VMEM((ROWS, taken, width), jnp.float32),
+            pltpu.VMEM((width // LANES, taken * ROWS, LANES), jnp.float32),
             pltpu.VMEM((ROWS, n * send_max, width), jnp.float32),
             pltpu.VMEM((steps, count, rows, width), jnp.int16),
             pltpu.VMEM((steps, count, 1, LANES), jnp.float32),
@@ -788,10 +821,9 @@
         + [sem((steps, n))] * 2
         + [sem((n,))] * 2
         + [sem((steps, count))] * 4
-        + [sem((n,))] * 2
-        + [sem((7,))],
+        + [sem((steps, n)), sem((n,)), sem((7,))],
         compiler_params=pltpu.CompilerParams(
-            collective_id=1, has_side_effects=True, vmem_limit_bytes=54 << 20
+            collective_id=1, has_side_effects=True, vmem_limit_bytes=47 << 20
         ),
         name="fused",
     )(asked, pos, owners, slots_of, prolong, stiffness)
@@ -896,8 +928,7 @@
     halved = per_peer == group and gx % 2 == 0 and slots == LANES and cv % ROWS == 0 and 2 * group == ROWS == 2 * send_max and 2 * each + own_aggs <= LANES
 
     if halved:
-        owners = jnp.pad(coarse_owner.T, ((0, 0), (2 * each, LANES - own_aggs - 2 * each)))
-        held = (request[None], col_pos.T, owners, col_slot.T, prolong, stiffness)
+        held = (request[None], col_pos.T, coarse_owner.T, col_slot.T, prolong, stiffness)
         held = [pltpu.with_memory_space_constraint(a, pltpu.HBM) for a in held]
         return fused(*held, gx, gy, group, send_max)
     meta = jnp.concatenate([request.reshape(n, per_peer), col_pos.reshape(n, per_peer * bps)], axis=1)

time: 101 us -> 95.4 us (0.945)
  the two profiles are of different devices: /device:TPU:11 before, /device:TPU:1 now
where the time goes in v3:
time: 95.4 us; the launch traced here: 95.3 us
  Pallas kernels  93.1 us (98%)
  local copies, waits for them, and re-layouts  2.19 us (2%)
    pallas_call x1, Pallas kernels, fused(): pl.pallas_call(functools.partial(fused_kernel, (gx, gy, cv, bps, group, s...  93.1 us
    unnamed x1, local copies, waits for them, and re-layouts  2.19 us

profile of v3, /device:TPU:1, one launch (start us, length us, event | category | flops | bytes accessed | tf_op | source)
XLA Modules:
  0.0 95.3 jit_solution(11863236390928369667)
XLA Ops:
  0.0 93.1 %fused.1 = f32[128,24,384]{2,1,0:T(8,128)S(1)} custom-call(s32[1,128]{1,0:T(1,128)} %bitcast.6, s32[4,128]{1,0:T(4,128)} %bitcast.4, s32[1,64]{1,0:T(1,128)} %bitcast.7, s32[4,128]{1,0:T(4,128)} %bitcast.5, bf16[64,24,128]{2,1,0:T(8,128)(2,1)} %prolong_in.1, bf16[128,4,128,128]{3,2,1,0:T(8,128)(2,1)} %stiff_ref.1), custom_call_target="tpu_custom_call" | custom-call | tf_op jit(solution)/shard_map/fused/pallas_call | solution.py:786
  93.1 2.2 %copy.8 = f32[128,24,384]{2,1,0:T(8,128)} copy(f32[128,24,384]{2,1,0:T(8,128)S(1)} %fused.1) | data formatting | bytes 9437184

commit v4 on v3

--- a/solution.py
+++ b/solution.py
@@ -419,10 +419,10 @@
     def where(peer):
         return (peer // gy, lax.rem(peer, gy))
 
-    def remote(src, dst, send_sem, recv_sem, peer):
+    def remote(src, dst, send_sem, recv_sem, peer, device=None):
         return pltpu.make_async_remote_copy(
             src_ref=src, dst_ref=dst, send_sem=send_sem, recv_sem=recv_sem,
-            device_id=where(peer), device_id_type=MESH,
+            device_id=where(peer) if device is None else device, device_id_type=MESH,
         )
 
     def meta_copy(peer, source):
@@ -438,16 +438,18 @@
             fetch_send.at[peer], fetch_recv.at[source], peer,
         )
 
-    def part_copy(h, peer, source):
+    def part_copy(h, peer, source, at=None, device=None):
+        at = lax.rem(peer, count) if at is None else at
         return remote(
-            code_ref.at[lax.rem(peer, count), h], part_ref.at[source, h],
-            part_send.at[h, peer], part_recv.at[h, source], peer,
+            code_ref.at[at, h], part_ref.at[source, h],
+            part_send.at[h, peer], part_recv.at[h, source], peer, device,
         )
 
-    def scale_copy(peer, source):
+    def scale_copy(peer, source, at=None, device=None):
+        at = lax.rem(peer, count) if at is None else at
         return remote(
-            factor_ref.at[lax.rem(peer, count)], scale_ref.at[source],
-            scale_send.at[peer], scale_recv.at[source], peer,
+            factor_ref.at[at], scale_ref.at[source],
+            scale_send.at[peer], scale_recv.at[source], peer, device,
         )
 
     def row_copies(h, peer, source):
@@ -584,13 +586,16 @@
     lax.fori_loop(0, n - 1, take, 0)
 
     def send(h, j, both):
+        half = gx // 2
         i = lax.rem(j + 1, count)
-        far = offset_at(i, 1 - side, 1, gx, gy)
-        near = offset_at(i, side, 1, gx, gy)
-        for peer in (far, near) if both else (far,):
+        row = lax.rem(lax.rem(lax.axis_index("gx"), half) + i // gy, half)
+        col = lax.rem(lax.axis_index("gy") + lax.rem(i, gy), gy)
+        at = row * gy + col
+        for there in (1 - side, side) if both else (1 - side,):
+            spot = (there * count + at, at, (there * half + row, col))
             if h == 0:
-                scale_copy(peer, me).start()
-            part_copy(h, peer, me).start()
+                scale_copy(spot[0], me, *spot[1:]).start()
+            part_copy(h, spot[0], me, *spot[1:]).start()
 
     def work(g, c):
         for v in range(DEEP):
@@ -742,10 +747,6 @@
             pack(u % count, u == count)
         for u in range(count - 2 * PAIR + 1, count):
             hand(u)
-        if h > 0:
-            decode_all(h - 1)
-    decode_all(steps - 1)
-
     def drain(k, c):
         peer = mixed_at(k, 1, gx, gy)
         fetch_copy(peer, me).wait_send()
@@ -754,15 +755,18 @@
             part_copy(h, peer, me).wait_send()
         return c
 
-    lax.fori_loop(0, n - 1, drain, 0)
-
-    def finish(i, c):
-        for h in range(steps):
-            for copy in row_copies(h, by_turn(i, 1), mine):
-                copy.wait_send()
-        return c
-
-    lax.fori_loop(1, count, finish, 0)
+    def finish(i, c, h):
+        for copy in row_copies(h, by_turn(i, 1), mine):
+            copy.wait_send()
+        return c
+
+    for h in range(steps):
+        if h == steps - 1:
+            lax.fori_loop(0, n - 1, drain, 0)
+            for w in range(h):
+                lax.fori_loop(1, count, functools.partial(finish, h=w), 0)
+        decode_all(h)
+    lax.fori_loop(1, count, functools.partial(finish, h=steps - 1), 0)
 
     def written(i, c):
         for h in range(steps):

time: 95.4 us -> 92.9 us (0.974)
  the two profiles are of different devices: /device:TPU:1 before, /device:TPU:11 now
where the time goes in v4:
time: 92.9 us; the launch traced here: 91.7 us
  Pallas kernels  89.5 us (96%)
  local copies, waits for them, and re-layouts  2.19 us (2%)
    pallas_call x1, Pallas kernels, fused(): pl.pallas_call(functools.partial(fused_kernel, (gx, gy, cv, bps, group, s...  89.5 us
    unnamed x1, local copies, waits for them, and re-layouts  2.19 us

profile of v4, /device:TPU:11, one launch (start us, length us, event | category | flops | bytes accessed | tf_op | source)
XLA Modules:
  0.0 91.7 jit_solution(1252144751803960656)
XLA Ops:
  0.0 89.5 %fused.1 = f32[128,24,384]{2,1,0:T(8,128)S(1)} custom-call(s32[1,128]{1,0:T(1,128)} %bitcast.6, s32[4,128]{1,0:T(4,128)} %bitcast.4, s32[1,64]{1,0:T(1,128)} %bitcast.7, s32[4,128]{1,0:T(4,128)} %bitcast.5, bf16[64,24,128]{2,1,0:T(8,128)(2,1)} %prolong_in.1, bf16[128,4,128,128]{3,2,1,0:T(8,128)(2,1)} %stiff_ref.1), custom_call_target="tpu_custom_call" | custom-call | tf_op jit(solution)/shard_map/fused/pallas_call | solution.py:790
  89.5 2.2 %copy.8 = f32[128,24,384]{2,1,0:T(8,128)} copy(f32[128,24,384]{2,1,0:T(8,128)S(1)} %fused.1) | data formatting | bytes 9437184

commit v5 on v4

--- a/solution.py
+++ b/solution.py
@@ -548,17 +548,18 @@
         peer = mixed_at(k, 1, gx, gy)
         for j in range(group):
             stage_ref[peer * group + j] = prolong_ref[req_ref[peer, 0, first + j]]
+
+        @pl.when(k > 0)
+        def _():
+            fetch_copy(mixed_at(k - 1, 1, gx, gy), me).start()
+
         return c
 
     lax.fori_loop(0, n - 1, fill, 0)
+    fetch_copy(mixed_at(n - 2, 1, gx, gy), me).start()
     for j in range(group):
         stage_ref[me * group + j] = prolong_ref[req_ref[me, 0, first + j]]
 
-    def answer(k, c):
-        fetch_copy(mixed_at(k, 1, gx, gy), me).start()
-        return c
-
-    lax.fori_loop(0, n - 1, answer, 0)
 
     def project(source, from_ref):
         mats_copy(source).wait()

time: 92.9 us -> 92.1 us (level)
  no operation moved by 1% of the time
where the time goes in v5:
time: 92.1 us; the launch traced here: 90.8 us
  Pallas kernels  88.6 us (96%)
  local copies, waits for them, and re-layouts  2.19 us (2%)
    pallas_call x1, Pallas kernels, fused(): pl.pallas_call(functools.partial(fused_kernel, (gx, gy, cv, bps, group, s...  88.6 us
    unnamed x1, local copies, waits for them, and re-layouts  2.19 us

profile of v5, /device:TPU:11, one launch (start us, length us, event | category | flops | bytes accessed | tf_op | source)
XLA Modules:
  0.0 90.8 jit_solution(6806264976686010556)
XLA Ops:
  0.0 88.6 %fused.1 = f32[128,24,384]{2,1,0:T(8,128)S(1)} custom-call(s32[1,128]{1,0:T(1,128)} %bitcast.6, s32[4,128]{1,0:T(4,128)} %bitcast.4, s32[1,64]{1,0:T(1,128)} %bitcast.7, s32[4,128]{1,0:T(4,128)} %bitcast.5, bf16[64,24,128]{2,1,0:T(8,128)(2,1)} %prolong_in.1, bf16[128,4,128,128]{3,2,1,0:T(8,128)(2,1)} %stiff_ref.1), custom_call_target="tpu_custom_call" | custom-call | tf_op jit(solution)/shard_map/fused/pallas_call | solution.py:791
  88.6 2.2 %copy.8 = f32[128,24,384]{2,1,0:T(8,128)} copy(f32[128,24,384]{2,1,0:T(8,128)S(1)} %fused.1) | data formatting | bytes 9437184
